TPU v7x, 32 devices: a whole 2x2x4 slice. The times are simulated.
32 devices in a mesh: col: 8 (over y, x, core), row: 4 (over z).
Axes of the slice: x: 2, y: 2, z: 4, core: 2. Of those that a mesh axis runs over, the one named last changes fastest.
Arguments:
- trace_start: float32 [32, 32768], P(None, ('col', 'row')), may hold values from -6 to 6
- surface_load: float32 [32, 32768], P(None, ('col', 'row')), may hold values from -6 to 6
- panel_tiles: bfloat16 [704, 512, 512], P(('col', 'row')), may hold values from -0.03125 to 0.03125
- tile_list: int32 [704], P(('col', 'row')), may hold values from -1 to 4095, as said below
- surf_map: int32 [8], replicated, may hold values from 0 to 7, as said below
- coef_index: int32 [2, 4, 16384], P(None, None, 'row'), may hold values from 0 to 15
- coef_table: float32 [16], replicated, may hold values from 0.2 to 2
- vol_source: float32 [2, 4, 16384], P(None, None, 'row'), may hold values from -6 to 6
Outputs:
- traces: float32 [32, 32768], P(None, ('col', 'row'))
- response: float32 [32, 32768], P(None, ('col', 'row'))
Inputs may be any that keep to these rules, and one draw needn't show every extreme that they name: `tile_list`: each device has 22 slots, ordered by col index, then row index, then slot. A value i * 64 + j names the tile of rows i * 512 to (i + 1) * 512 - 1 and columns j * 512 to (j + 1) * 512 - 1 of the boundary matrix, with j <= i and j < 8; each such tile is named exactly once. A device of col index c and row index r names only tiles whose rows lie in shards of row index r (i * 512 // 1024 leaves remainder r modulo 4), and none if c >= 6; its named tiles fill its first slots and the rest hold -1. Some device names 22 tiles. surf_map[r * 2 + q] leaves remainder r modulo 4; each volume tile lies under exactly one surface tile.
All inputs are finite; a program needn't handle non-finite values.
Results may differ from a plain program's by a relative error of at most 0.0041.
Values may be sent and summed in bfloat16 or wider, within the bound.
A program may use at most 128 MiB of HBM per device.

v0:
```python
import functools

import jax
import jax.numpy as jnp
from jax import lax
from jax.experimental import pallas as pl
from jax.experimental.pallas import tpu as pltpu
from jax.sharding import PartitionSpec as P

ITERS = 2
SWEEPS = 4

COUPLING_STEP = 0.3
JACOBI_WEIGHT = 0.8
CELL_MASS = 0.05

LANES = 128
SUB = 8
F32 = jnp.float32
BF16 = jnp.bfloat16


def kernel(
    cfg,
    row_tile_ref,
    col_tile_ref,
    slot_ref,
    surf_ref,
    table_ref,
    start_ref,
    load_ref,
    index_ref,
    source_ref,
    panel_hbm,
    traces_ref,
    response_ref,
    panel,
    own,
    band,
    window,
    edge_left,
    edge_right,
    halo_index,
    halo_source,
    product,
    window_part,
    window_recv,
    row_part,
    row_recv,
    coef_ext,
    source_ext,
    weights,
    state,
    top,
    panel_sem,
    band_send,
    band_recv,
    win_send,
    win_recv,
    edge_send,
    edge_recv,
    halo_send,
    halo_recv,
    part_send,
    part_recv,
    row_send,
    row_rsem,
    band_now,
    window_now,
    edge_now,
):
    cols, rows, lines, per_shard, tile, slots, nodes, layers, rhs, levels = cfg
    dense = cols - lines
    group = cols // lines
    shard = per_shard * tile
    win_tiles = rows * per_shard
    c = lax.axis_index("col")
    r = lax.axis_index("row")
    vol = jnp.maximum(c - dense, 0)
    row_up = jnp.minimum(r + 1, rows - 1)
    row_down = jnp.maximum(r - 1, 0)
    is_volume = c >= dense
    is_dense = c < dense
    first_of_tile = (lax.rem(c, group) == 0) & (r > 0)
    last_of_tile = (lax.rem(c, group) == group - 1) & (r < rows - 1)
    has_left = r > 0
    has_right = r < rows - 1

    def copy(src, dst, send, recv, to_col, to_row):
        return pltpu.make_async_remote_copy(
            src_ref=src,
            dst_ref=dst,
            send_sem=send,
            recv_sem=recv,
            device_id=(to_col, to_row),
            device_id_type=pl.DeviceIdType.MESH,
        )

    def col_peer(k):
        return lax.rem(c + k, cols)

    def row_peer(k):
        return lax.rem(r + k, rows)

    def panel_copy(s):
        return pltpu.make_async_copy(panel_hbm.at[s], panel.at[s], panel_sem.at[s])

    @pl.when(is_dense)
    def _():
        def start(s, _):
            panel_copy(s).start()
            return 0

        lax.fori_loop(0, slots, start, 0)

    barrier = pltpu.get_barrier_semaphore()

    def greet(to_col, to_row):
        pl.semaphore_signal(
            barrier, inc=1, device_id=(to_col, to_row), device_id_type=pl.DeviceIdType.MESH
        )

    for k in range(1, cols):
        greet(col_peer(k), r)
    for k in range(1, rows):
        greet(c, row_peer(k))

    @pl.when(last_of_tile)
    def _():
        for v in range(lines):
            greet(dense + v, row_up)

    @pl.when(first_of_tile)
    def _():
        for v in range(lines):
            greet(dense + v, row_down)

    @pl.when(is_volume & has_left)
    def _():
        for q in range(lines):
            greet(q * group + group - 1, row_down)

    @pl.when(is_volume & has_right)
    def _():
        for q in range(lines):
            greet(q * group, row_up)

    def count(flag):
        return jnp.where(flag, lines, 0)

    expected = (
        cols
        - 1
        + rows
        - 1
        + count(last_of_tile)
        + count(first_of_tile)
        + count(is_volume & has_left)
        + count(is_volume & has_right)
    )
    traces_ref[...] = start_ref[...]
    product[slots] = jnp.zeros((rhs, tile), F32)
    pl.semaphore_wait(barrier, expected)

    def halo_copy(kind, side, arrival=False):
        ref = (index_ref, source_ref)[kind]
        dst = (halo_index, halo_source)[kind]
        at = nodes - LANES if side == 0 else 0
        to = row_up if (side == 0) != arrival else row_down
        return copy(
            ref.at[:, :, pl.ds(at, LANES)],
            dst.at[side],
            halo_send.at[kind, side],
            halo_recv.at[kind, side],
            c,
            to,
        )

    sides = ((0, has_right, has_left), (1, has_left, has_right))
    for side, sends, _ in sides:

        @pl.when(is_volume & sends)
        def _():
            for kind in range(2):
                halo_copy(kind, side).start()

    def band_copy(it, k):
        to = col_peer(k)
        return copy(own.at[it], band.at[it, c], band_send.at[it, k], band_recv.at[it, c], to, r)

    def band_arrival(it, src):
        return copy(own.at[it], band.at[it, src], band_send.at[it, 0], band_recv.at[it, src], src, r)

    def edge_copy(it, side, v):
        q = lax.div(c, group)
        if side == 0:
            src = own.at[it, per_shard - 1, :, pl.ds(tile - LANES, LANES)]
            dst, to = edge_left, row_up
        else:
            src = own.at[it, 0, :, pl.ds(0, LANES)]
            dst, to = edge_right, row_down
        return copy(
            src,
            dst.at[it, q],
            edge_send.at[it, side, v],
            edge_recv.at[it, side, q],
            dense + v,
            to,
        )

    def edge_arrival(it, side, q):
        dst = (edge_left, edge_right)[side]
        src = own.at[it, 0, :, pl.ds(0, LANES)]
        if side == 0:
            from_col, from_row = q * group + group - 1, row_down
        else:
            from_col, from_row = q * group, row_up
        return copy(
            src,
            dst.at[it, q],
            edge_send.at[it, side, 0],
            edge_recv.at[it, side, q],
            from_col,
            from_row,
        )

    def window_copy(it, k):
        to = row_peer(k)
        return copy(band.at[it, 0], window.at[it, r], win_send.at[it, k], win_recv.at[it, r], c, to)

    def window_arrival(it, k):
        src = row_peer(k)
        return copy(
            band.at[it, 0], window.at[it, src], win_send.at[it, k], win_recv.at[it, src], c, src
        )

    def part_copy(it, k):
        to = row_peer(k)
        return copy(
            window_part.at[it, to],
            window_recv.at[it, r],
            part_send.at[it, k],
            part_recv.at[it, r],
            c,
            to,
        )

    def part_arrival(it, k):
        src = row_peer(k)
        return copy(
            window_part.at[it, src],
            window_recv.at[it, src],
            part_send.at[it, k],
            part_recv.at[it, src],
            c,
            src,
        )

    def row_copy(it, to):
        return copy(
            row_part.at[it, to], row_recv.at[it, c], row_send.at[it, to], row_rsem.at[it, c], to, r
        )

    def row_arrival(it, src):
        return copy(
            row_part.at[it, src],
            row_recv.at[it, src],
            row_send.at[it, src],
            row_rsem.at[it, src],
            src,
            r,
        )

    def prepare_volume():
        line = lax.div(surf_ref[r * lines + vol], rows)
        padded = nodes + 4 * LANES
        for side, _, receives in sides:

            @pl.when(receives)
            def _():
                for kind in range(2):
                    halo_copy(kind, side, True).wait_recv()

            @pl.when(jnp.logical_not(receives))
            def _():
                halo_index[side] = jnp.zeros((lines, layers, LANES), jnp.int32)
                halo_source[side] = jnp.zeros((lines, layers, LANES), F32)

        def lookup(indices):
            values = jnp.zeros(indices.shape, F32)
            for level in range(levels):
                values = jnp.where(indices == level, table_ref[level], values)
            return values

        zeros = jnp.zeros((layers, LANES), F32)
        left_on = jnp.where(has_left, 1.0, 0.0)
        right_on = jnp.where(has_right, 1.0, 0.0)
        right_at = 2 * LANES + nodes
        coef_ext[:, 0:LANES] = zeros
        coef_ext[:, LANES : 2 * LANES] = lookup(halo_index[0, line]) * left_on
        coef_ext[:, 2 * LANES : right_at] = lookup(index_ref[line])
        coef_ext[:, right_at : right_at + LANES] = lookup(halo_index[1, line]) * right_on
        coef_ext[:, right_at + LANES :] = zeros
        source_ext[:, 0:LANES] = zeros
        source_ext[:, LANES : 2 * LANES] = halo_source[0, line]
        source_ext[:, 2 * LANES : right_at] = source_ref[line]
        source_ext[:, right_at : right_at + LANES] = halo_source[1, line]
        source_ext[:, right_at + LANES :] = zeros
        lane = lax.broadcasted_iota(jnp.int32, (1, padded), 1)
        low = jnp.where(has_left, LANES, 2 * LANES)
        high = jnp.where(has_right, right_at + LANES, right_at)
        inside = (lane >= low) & (lane < high)
        for layer in range(layers):
            k = coef_ext[layer : layer + 1, :]
            left = 0.5 * (k + pltpu.roll(k, 1, 1))
            right = 0.5 * (k + pltpu.roll(k, padded - 1, 1))
            up = 0.5 * (k + coef_ext[layer - 1 : layer, :]) if layer else k
            diagonal = left + right + up + CELL_MASS
            parts = [left, right, up]
            if layer < layers - 1:
                down = 0.5 * (k + coef_ext[layer + 1 : layer + 2, :])
                diagonal = diagonal + down
                parts.append(down)
            else:
                parts.append(None)
            parts.append(source_ext[layer : layer + 1, :])
            scale = jnp.where(inside, JACOBI_WEIGHT / diagonal, 0.0)
            for kind, part in enumerate(parts):
                if part is not None:
                    weights[kind, layer] = jnp.broadcast_to(part * scale, (SUB, padded))
        top[:, 0:LANES] = jnp.zeros((rhs, LANES), F32)
        top[:, right_at + LANES :] = jnp.zeros((rhs, LANES), F32)
        for layer in range(layers):
            state[0, layer] = jnp.zeros((rhs, padded), F32)
            state[1, layer, :, 0:LANES] = jnp.zeros((rhs, LANES), F32)
            state[1, layer, :, right_at + LANES :] = jnp.zeros((rhs, LANES), F32)

    def relax(now, at, width):
        span = width + 2 * LANES
        begin = pl.multiple_of(at - LANES, LANES)
        at = pl.multiple_of(at, LANES)
        for layer in range(layers):
            factors = [
                None if kind == 3 and layer == layers - 1 else weights[kind, layer, :, pl.ds(at, width)]
                for kind in range(5)
            ]
            for g in range(rhs // SUB):
                lines_at = pl.ds(g * SUB, SUB)
                around = state[now, layer, lines_at, pl.ds(begin, span)]
                centre = around[:, LANES : LANES + width]
                before = pltpu.roll(around, 1, 1)[:, LANES : LANES + width]
                after = pltpu.roll(around, span - 1, 1)[:, LANES : LANES + width]
                if layer:
                    above = state[now, layer - 1, lines_at, pl.ds(at, width)]
                else:
                    above = top[lines_at, pl.ds(at, width)]
                value = (1.0 - JACOBI_WEIGHT) * centre + factors[4]
                value = value + factors[0] * before + factors[1] * after + factors[2] * above
                if layer < layers - 1:
                    value = value + factors[3] * state[now, layer + 1, lines_at, pl.ds(at, width)]
                state[1 - now, layer, lines_at, pl.ds(at, width)] = value

    def volume(it):
        q = vol
        right_at = 2 * LANES + nodes
        for m in range(group):
            src = q * group + m

            @pl.when(src != c)
            def _():
                band_arrival(it, src).wait_recv()

            for p in range(per_shard):
                at = 2 * LANES + m * shard + p * tile
                top[:, at : at + tile] = band[it, src, p].astype(F32)
        line = lax.div(surf_ref[r * lines + q], rows)
        for side, _, receives in sides:
            dst = (edge_left, edge_right)[side]
            at = LANES if side == 0 else right_at
            base = row_down if side == 0 else row_up
            place = 0
            for z in range(lines):
                place = jnp.where(surf_ref[base * lines + z] == line * rows + base, z, place)

            @pl.when(receives)
            def _():
                for z in range(lines):
                    edge_arrival(it, side, z).wait_recv()
                for z in range(lines):
                    edge_now[z] = dst[it, z]
                top[:, at : at + LANES] = edge_now[place].astype(F32)

            @pl.when(jnp.logical_not(receives))
            def _():
                top[:, at : at + LANES] = jnp.zeros((rhs, LANES), F32)

        width = 2 * tile

        def sweep(now):
            relax(now, LANES, LANES)
            relax(now, right_at, LANES)

            def chunk(j, _):
                relax(now, 2 * LANES + j * width, width)
                return 0

            lax.fori_loop(0, nodes // width, chunk, 0)

        for i in range(SWEEPS):
            sweep(i % 2)
        done = SWEEPS % 2
        for m in range(group):
            to = q * group + m
            for p in range(per_shard):
                at = 2 * LANES + m * shard + p * tile
                k = index_coef(at)
                flux = k * (top[:, at : at + tile] - state[done, 0, :, at : at + tile])
                row_part[it, to, p] = flux.astype(BF16)

            @pl.when(to != c)
            def _():
                row_copy(it, to).start()

    def index_coef(at):
        return coef_ext[0:1, at : at + tile]

    def total_of(tiles_of):
        value = product[tiles_of[0]]
        for t in tiles_of[1:]:
            value = value + product[t]
        return value

    def dense_part(it):
        @pl.when(c != 0)
        def _():
            band_arrival(it, 0).wait_recv()

        for k in range(1, rows):
            window_copy(it, k).start()
        window[it, r] = band[it, 0]
        for src in range(1, cols):

            @pl.when(c != src)
            def _():
                band_arrival(it, src).wait_recv()

        for src in range(cols):
            band_now[src] = band[it, src]

        def into_cols(s, _):
            @pl.when(it == 0)
            def _():
                panel_copy(s).wait()

            row_tile = row_tile_ref[s]
            traces = band_now[lax.div(row_tile, per_shard), lax.rem(row_tile, per_shard)]
            product[s] = jnp.dot(traces, panel[s], preferred_element_type=F32)
            return 0

        lax.fori_loop(0, slots, into_cols, 0)
        band_tiles = cols * per_shard

        def sum_window(j, _):
            value = total_of([slot_ref[b * win_tiles + j] for b in range(band_tiles)])
            window_part[it, lax.div(j, per_shard), lax.rem(j, per_shard)] = value.astype(BF16)
            return 0

        lax.fori_loop(0, win_tiles, sum_window, 0)
        for k in range(1, rows):
            part_copy(it, k).start()
        for k in range(1, rows):
            window_arrival(it, k).wait_recv()

        for src in range(rows):
            window_now[src] = window[it, src]

        def into_rows(s, _):
            col_tile = col_tile_ref[s]
            traces = window_now[lax.div(col_tile, per_shard), lax.rem(col_tile, per_shard)]
            product[s] = lax.dot_general(
                traces, panel[s], (((1,), (1,)), ((), ())), preferred_element_type=F32
            )
            return 0

        lax.fori_loop(0, slots, into_rows, 0)

        def sum_rows(b, _):
            value = total_of([slot_ref[b * win_tiles + j] for j in range(win_tiles)])
            row_part[it, lax.div(b, per_shard), lax.rem(b, per_shard)] = value.astype(BF16)
            return 0

        lax.fori_loop(per_shard, band_tiles, sum_rows, 0)
        for to in range(1, cols):

            @pl.when(c != to)
            def _():
                row_copy(it, to).start()

        for k in range(1, rows):
            part_arrival(it, k).wait_recv()
        for p in range(per_shard):
            value = total_of([slot_ref[p * win_tiles + j] for j in range(win_tiles)])
            value = value + window_part[it, r, p].astype(F32)
            for k in range(1, rows):
                value = value + window_recv[it, row_peer(k), p].astype(F32)
            row_part[it, 0, p] = value.astype(BF16)

        @pl.when(c != 0)
        def _():
            row_copy(it, 0).start()

    def iteration(it, _):
        for p in range(per_shard):
            rounded = traces_ref[:, p * tile : (p + 1) * tile].astype(BF16)
            own[it, p] = rounded
            band[it, c, p] = rounded
        for k in range(1, cols):
            band_copy(it, k).start()
        for side, flag in ((0, last_of_tile), (1, first_of_tile)):

            @pl.when(flag)
            def _():
                for v in range(lines):
                    edge_copy(it, side, v).start()

        @pl.when(is_volume)
        def _():
            @pl.when(it == 0)
            def _():
                prepare_volume()

            volume(it)
            for k in range(cols):

                @pl.when((k != c) & (k // group != c - dense))
                def _():
                    band_arrival(it, k).wait_recv()

        @pl.when(is_dense)
        def _():
            dense_part(it)

        owner = dense + lax.div(c, group)
        for src in range(cols):

            @pl.when((src != c) & ((src < dense) | (src == owner)))
            def _():
                row_arrival(it, src).wait_recv()

        def own_part(p):
            return row_part[it, c, p].astype(F32)

        for p in range(per_shard):
            at = slice(p * tile, (p + 1) * tile)
            response_ref[:, at] = jnp.zeros((rhs, tile), F32)
            for src in range(dense):

                @pl.when(src != c)
                def _():
                    response_ref[:, at] += row_recv[it, src, p].astype(F32)

            @pl.when(owner != c)
            def _():
                response_ref[:, at] += row_recv[it, owner, p].astype(F32)

            @pl.when(is_dense | (owner == c))
            def _():
                response_ref[:, at] += own_part(p)

            t = traces_ref[:, at]
            traces_ref[:, at] = t + COUPLING_STEP * (load_ref[:, at] - t - response_ref[:, at])
        return 0

    lax.fori_loop(0, ITERS, iteration, 0)

    def drain(it, _):
        for k in range(1, cols):
            band_copy(it, k).wait_send()
        for side, flag in ((0, last_of_tile), (1, first_of_tile)):

            @pl.when(flag)
            def _():
                for v in range(lines):
                    edge_copy(it, side, v).wait_send()

        @pl.when(is_dense)
        def _():
            for k in range(1, rows):
                window_copy(it, k).wait_send()
                part_copy(it, k).wait_send()
            for to in range(cols):

                @pl.when(c != to)
                def _():
                    row_copy(it, to).wait_send()

        @pl.when(is_volume)
        def _():
            for m in range(group):
                to = vol * group + m

                @pl.when(to != c)
                def _():
                    row_copy(it, to).wait_send()

        return 0

    lax.fori_loop(0, ITERS, drain, 0)
    for side, sends, _ in sides:

        @pl.when(is_volume & sends)
        def _():
            for kind in range(2):
                halo_copy(kind, side).wait_send()


def local(
    trace_start, surface_load, panel_tiles, tile_list, surf_map, coef_index, coef_table, vol_source
):
    cols = lax.axis_size("col")
    rows = lax.axis_size("row")
    row_index = lax.axis_index("row")
    lines, layers, nodes = coef_index.shape
    slots, tile, _ = panel_tiles.shape
    rhs, shard = trace_start.shape
    per_shard = shard // tile
    levels = coef_table.shape[0]
    side = cols * rows * per_shard
    band_tiles = cols * per_shard
    win_tiles = rows * per_shard
    safe = jnp.maximum(tile_list, 0)
    row_tile = safe // side
    col_tile = safe % side
    band_tile = row_tile // per_shard // rows * per_shard + row_tile % per_shard
    b = jnp.arange(band_tiles, dtype=jnp.int32)
    name_row = (b // per_shard * rows + row_index) * per_shard + b % per_shard
    names = (name_row[:, None] * side + jnp.arange(win_tiles, dtype=jnp.int32)).reshape(-1)
    order = jnp.arange(slots, dtype=jnp.int32)
    slot_table = slots - jnp.max(
        jnp.where(names[:, None] == tile_list[None, :], slots - order, 0), axis=1
    )
    padded = nodes + 4 * LANES
    cfg = (cols, rows, lines, per_shard, tile, slots, nodes, layers, rhs, levels)
    smem = pl.BlockSpec(memory_space=pltpu.SMEM)
    vmem = pl.BlockSpec(memory_space=pltpu.VMEM)
    block = (per_shard, rhs, tile)
    dma = pltpu.SemaphoreType.DMA
    out = jax.ShapeDtypeStruct((rhs, shard), F32)
    return pl.pallas_call(
        functools.partial(kernel, cfg),
        out_shape=(out, out),
        in_specs=[smem] * 5 + [vmem] * 4 + [pl.BlockSpec(memory_space=pl.ANY)],
        out_specs=(vmem, vmem),
        scratch_shapes=[
            pltpu.VMEM((slots, tile, tile), BF16),
            pltpu.VMEM((ITERS,) + block, BF16),
            pltpu.VMEM((ITERS, cols) + block, BF16),
            pltpu.VMEM((ITERS, rows) + block, BF16),
            pltpu.VMEM((ITERS, lines, rhs, LANES), BF16),
            pltpu.VMEM((ITERS, lines, rhs, LANES), BF16),
            pltpu.VMEM((2, lines, layers, LANES), jnp.int32),
            pltpu.VMEM((2, lines, layers, LANES), F32),
            pltpu.VMEM((slots + 1, rhs, tile), F32),
            pltpu.VMEM((ITERS, rows) + block, BF16),
            pltpu.VMEM((ITERS, rows) + block, BF16),
            pltpu.VMEM((ITERS, cols) + block, BF16),
            pltpu.VMEM((ITERS, cols) + block, BF16),
            pltpu.VMEM((layers, padded), F32),
            pltpu.VMEM((layers, padded), F32),
            pltpu.VMEM((5, layers, SUB, padded), F32),
            pltpu.VMEM((2, layers, rhs, padded), F32),
            pltpu.VMEM((rhs, padded), F32),
            dma((slots,)),
            dma((ITERS, cols)),
            dma((ITERS, cols)),
            dma((ITERS, rows)),
            dma((ITERS, rows)),
            dma((ITERS, 2, lines)),
            dma((ITERS, 2, lines)),
            dma((2, 2)),
            dma((2, 2)),
            dma((ITERS, rows)),
            dma((ITERS, rows)),
            dma((ITERS, cols)),
            dma((ITERS, cols)),
            pltpu.VMEM((cols,) + block, BF16),
            pltpu.VMEM((rows,) + block, BF16),
            pltpu.VMEM((lines, rhs, LANES), BF16),
        ],
        compiler_params=pltpu.CompilerParams(
            collective_id=0, has_side_effects=True, vmem_limit_bytes=60 * 1024 * 1024
        ),
        name="coupled",
    )(
        band_tile,
        col_tile,
        slot_table,
        surf_map,
        coef_table,
        trace_start,
        surface_load,
        coef_index,
        vol_source,
        panel_tiles,
    )


def solution(mesh):
    return jax.shard_map(
        local,
        mesh=mesh,
        in_specs=(
            P(None, ("col", "row")),
            P(None, ("col", "row")),
            P(("col", "row"), None, None),
            P(("col", "row")),
            P(),
            P(None, None, "row"),
            P(),
            P(None, None, "row"),
        ),
        out_specs=(P(None, ("col", "row")), P(None, ("col", "row"))),
        check_vma=False,
    )
```

profile of v0, /device:TPU:0, one launch (start us, length us, event | category | flops | bytes accessed | tf_op | source)
XLA Modules:
  0.0 86.2 jit_solution(3795848848002160535)
XLA Ops:
  0.7 1.2 %and_select_fusion.2 = (s32[22]{0:T(128)}, s32[22]{0:T(128)}) fusion(s32[22]{0:T(128)} %param.11), kind=kLoop, calls=%fused_computation.4 | loop fusion | flops 1078 | bytes 264 | tf_op jit(solution)/shard_map/jit(remainder)/select_n | solution.py:633
  1.8 0.1 iota_add_fusion
  1.9 0.1 add.78
  2.0 0.7 select_reduce_fusion
  2.8 0.6 broadcast_subtract_fusion.slot_ref
  3.3 79.7 %coupled.1 = (f32[32,1024]{1,0:T(8,128)}, f32[32,1024]{1,0:T(8,128)}) custom-call(s32[22]{0:T(128)} %get-tuple-element.3.row_tile_ref, s32[22]{0:T(128)} %get-tuple-element.2.col_tile_ref, s32[128]{0:T(128)} %broadcast_subtract_fusion.slot_ref, s32[8]{0:T(128)} %surf_ref.1, f32[16]{0:T(128)} %table_ref.1, f32[32,1024]{1,0:T(8,128)} %start_ref.1, ...), custom_call_target="tpu_custom_call" | custom-call | tf_op jit(solution)/shard_map/coupled/pallas_call | solution.py:649
  83.0 1.6 %copy.12 = f32[32,1024]{1,0:T(8,128)} copy(f32[32,1024]{1,0:T(8,128)} %get-tuple-element.6) | data formatting | bytes 262144
  84.6 1.6 %copy.13 = f32[32,1024]{1,0:T(8,128)} copy(f32[32,1024]{1,0:T(8,128)} %get-tuple-element.7) | data formatting | bytes 262144
  (2 shorter events, 0.0 us)
where the time goes:
time: 86.4 us; the launch traced here: 86.2 us
  Pallas kernels  79.7 us (92%)
  local copies, waits for them, and re-layouts  3.22 us (4%)
  other arithmetic  2.6 us (3%)
    pallas_call x1, Pallas kernels, local(): pl.pallas_call(functools.partial(kernel, cfg), out_shape=(out, out), in_s...  79.7 us
    unnamed x2, local copies, waits for them, and re-layouts  3.14 us

commit v1 on v0

v1 whole, which is shorter than its diff:
```python
import functools

import jax
import jax.numpy as jnp
from jax import lax
from jax.experimental import pallas as pl
from jax.experimental.pallas import tpu as pltpu
from jax.sharding import PartitionSpec as P

ITERS = 2
SWEEPS = 4

COUPLING_STEP = 0.3
JACOBI_WEIGHT = 0.8
CELL_MASS = 0.05

LANES = 128
SUB = 8
CORES = 2
F32 = jnp.float32
BF16 = jnp.bfloat16
I32 = jnp.int32


def quotient(x, n):
    return x >> (n.bit_length() - 1) if n & (n - 1) == 0 else lax.div(x, n)


def remainder(x, n):
    return x & (n - 1) if n & (n - 1) == 0 else lax.rem(x, n)


def kernel(
    cfg,
    list_ref,
    surf_ref,
    table_ref,
    start_hbm,
    load_hbm,
    index_hbm,
    source_hbm,
    panel_hbm,
    traces_ref,
    response_ref,
    panel,
    load_ref,
    index_ref,
    source_ref,
    tab,
    order,
    band0,
    band1,
    window0,
    window1,
    edge_left,
    edge_right,
    halo_index,
    halo_source,
    product,
    mix_out,
    mix_in,
    zone_own,
    zone_out,
    zone_in,
    total_out,
    total_in,
    pair_out,
    pair_in,
    row_own,
    row_out,
    row_in,
    index_ext,
    coef_ext,
    source_ext,
    weights,
    state,
    top,
    flux,
    panel_sem,
    input_sem,
    tab_sem,
    band_send,
    pass_send,
    band_recv,
    win_send,
    win_pass,
    win_recv,
    edge_send,
    edge_recv,
    halo_send,
    halo_recv,
    mix_send,
    mix_recv,
    zone_send,
    zone_recv,
    total_send,
    total_recv,
    pair_send,
    pair_recv,
    row_send,
    row_recv,
):
    cols, rows, lines, per_shard, tile, slots, nodes, layers, rhs, levels = cfg
    dense = cols - lines
    group = cols // lines
    shard = per_shard * tile
    half = per_shard // CORES
    chips = cols // CORES
    dense_chips = dense // CORES
    win_tiles = rows * per_shard
    band_tiles = cols * per_shard
    side = cols * rows * per_shard
    span = shard + 2 * LANES
    bands = (band0, band1)
    windows = (window0, window1)
    c = lax.axis_index("col")
    r = lax.axis_index("row")
    core = lax.rem(c, CORES)
    chip = lax.div(c, CORES)
    other = 1 - core
    partner = chip * CORES + other
    q = lax.div(c, group)
    m = lax.rem(c, group)
    is_dense = c < dense
    row_up = jnp.minimum(r + 1, rows - 1)
    row_down = jnp.maximum(r - 1, 0)
    first_of_tile = m == 0
    last_of_tile = m == group - 1
    cross_left = first_of_tile & (r > 0)
    cross_right = last_of_tile & (r < rows - 1)

    def copy(src, dst, send, recv, to_col, to_row):
        return pltpu.make_async_remote_copy(
            src_ref=src,
            dst_ref=dst,
            send_sem=send,
            recv_sem=recv,
            device_id=(to_col, to_row),
            device_id_type=pl.DeviceIdType.MESH,
        )

    def panel_copy(s):
        return pltpu.make_async_copy(panel_hbm.at[s], panel.at[s], panel_sem.at[s])

    inputs = (
        (start_hbm, traces_ref),
        (index_hbm, index_ref),
        (source_hbm, source_ref),
        (load_hbm, load_ref),
    )

    def input_copy(i):
        return pltpu.make_async_copy(inputs[i][0], inputs[i][1], input_sem.at[i])

    for i in range(len(inputs)):
        input_copy(i).start()

    barrier = pltpu.get_barrier_semaphore()

    def greet(to_col, to_row):
        pl.semaphore_signal(
            barrier, inc=1, device_id=(to_col, to_row), device_id_type=pl.DeviceIdType.MESH
        )

    for k in range(1, rows):
        greet(c, lax.rem(r + k, rows))
    for k in range(1, cols):
        greet(lax.rem(c + k, cols), r)

    @pl.when(cross_right)
    def _():
        for z in range(lines):
            greet(z * group, row_up)

    @pl.when(cross_left)
    def _():
        for z in range(lines):
            greet(z * group + group - 1, row_down)

    @pl.when(is_dense)
    def _():
        def start(s, _):
            panel_copy(s).start()
            return 0

        lax.fori_loop(0, slots, start, 0)


    padded_slots = -(-slots // SUB) * SUB
    lane = lax.broadcasted_iota(I32, (SUB, LANES), 1)

    def sort_slots():
        slot = lax.broadcasted_iota(I32, (padded_slots, LANES), 0)
        lanes = lax.broadcasted_iota(I32, (padded_slots, LANES), 1)
        row_key = jnp.full((padded_slots, LANES), band_tiles, I32)
        col_key = jnp.full((padded_slots, LANES), win_tiles, I32)
        keys = []
        for s in range(slots):
            name = list_ref[s]
            safe = jnp.maximum(name, 0)
            row = quotient(safe, side)
            row = quotient(quotient(row, per_shard), rows) * per_shard + remainder(row, per_shard)
            row = jnp.where(name >= 0, row, band_tiles)
            col = jnp.where(name >= 0, remainder(safe, side), win_tiles)
            keys.append((col, row))
            row_key = jnp.where(slot == s, row, row_key)
            col_key = jnp.where(slot == s, col, col_key)

        def fold(x):
            x = functools.reduce(jnp.add, [x[i : i + SUB] for i in range(0, padded_slots, SUB)])
            for shift in (4, 2, 1):
                x = x + pltpu.roll(x, shift, 0)
            return x

        for which, key, source, count in (
            (0, col_key, row_key, win_tiles),
            (1, row_key, col_key, band_tiles),
        ):
            rank = jnp.zeros((padded_slots, LANES), I32)
            upto = jnp.zeros((SUB, LANES), I32)
            equal = jnp.zeros((SUB, LANES), I32)
            for s in range(slots):
                value = keys[s][which]
                ahead = (key > value) | ((key == value) & (slot > s))
                rank = rank + jnp.where(ahead, 1, 0)
                upto = upto + jnp.where(lane >= value, 1, 0)
                equal = equal + jnp.where(lane == value, 1, 0)
            rank = jnp.where(slot < slots, rank, LANES)
            here = rank == lanes
            place = fold(jnp.where(here, slot, 0))
            origin = fold(jnp.where(here, jnp.where(key < count, source, 0), 0))
            value = fold(jnp.where(here, key, 0))
            keep = (value == pltpu.roll(value, 1, 1)) & (lane > 0)
            last = jnp.where(equal > 0, upto - 1, slots)
            for i, x in enumerate((place, origin, jnp.where(keep, 1, 0), last)):
                tab[4 * which + i : 4 * which + i + 1, :] = x[0:1, :]

    @pl.when(is_dense)
    def _():
        sort_slots()
        pltpu.make_async_copy(tab, order, tab_sem).start()
        product[slots] = jnp.zeros((rhs, tile), F32)

    input_copy(0).wait()
    input_copy(1).wait()
    input_copy(2).wait()

    expected = (
        cols - 1 + rows - 1 + jnp.where(cross_right, lines, 0) + jnp.where(cross_left, lines, 0)
    )
    pl.semaphore_wait(barrier, expected)


    def halo_copy(kind, side_of, arrival=False):
        ref = (index_ref, source_ref)[kind]
        dst = (halo_index, halo_source)[kind]
        at = nodes - LANES if side_of == 0 else 0
        to = row_up if (side_of == 0) != arrival else row_down
        return copy(
            ref.at[:, :, pl.ds(at, LANES)],
            dst.at[side_of],
            halo_send.at[kind, side_of],
            halo_recv.at[kind, side_of],
            c,
            to,
        )

    halo_sends = (first_of_tile & (r < rows - 1), last_of_tile & (r > 0))
    halo_receives = (cross_left, cross_right)


    def edge_source(it, side_of):
        if side_of == 0:
            return bands[it].at[c * per_shard + per_shard - 1, :, pl.ds(tile - LANES, LANES)]
        return bands[it].at[c * per_shard, :, pl.ds(0, LANES)]

    def edge_near(it, side_of, arrival=False):
        dst = (edge_left, edge_right)[side_of]
        to = c + 1 if (side_of == 0) != arrival else c - 1
        return copy(
            edge_source(it, side_of),
            dst.at[it, lines],
            edge_send.at[it, side_of, lines],
            edge_recv.at[it, side_of, lines],
            to,
            r,
        )

    def edge_far(it, side_of, z):
        dst = (edge_left, edge_right)[side_of]
        to = (z * group, row_up) if side_of == 0 else (z * group + group - 1, row_down)
        return copy(
            edge_source(it, side_of),
            dst.at[it, q],
            edge_send.at[it, side_of, z],
            edge_recv.at[it, side_of, q],
            *to,
        )

    def edge_far_arrival(it, side_of, z):
        dst = (edge_left, edge_right)[side_of]
        at = (z * group + group - 1, row_down) if side_of == 0 else (z * group, row_up)
        return copy(
            edge_source(it, side_of),
            dst.at[it, z],
            edge_send.at[it, side_of, z],
            edge_recv.at[it, side_of, z],
            *at,
        )


    def shard_of(ref, col):
        return ref.at[pl.ds(col * per_shard, per_shard)]

    def peer_chip(k):
        return lax.rem(chip + k, chips)

    def band_copy(it, k, arrival=False):
        peer = peer_chip(k) * CORES + core
        at = peer if arrival else c
        return copy(
            shard_of(bands[it], at),
            shard_of(bands[it], at),
            band_send.at[it, k],
            band_recv.at[it, at],
            peer,
            r,
        )

    def band_pass(it, k, arrival=False):
        at = peer_chip(k) * CORES + (other if arrival else core)
        return copy(
            shard_of(bands[it], at),
            shard_of(bands[it], at),
            pass_send.at[it, k],
            band_recv.at[it, at],
            partner,
            r,
        )

    def window_copy(it, k, arrival=False):
        peer = lax.rem(r + k, rows)
        at = peer if arrival else r
        return copy(
            shard_of(bands[it], 0),
            shard_of(windows[it], at),
            win_send.at[it, k],
            win_recv.at[it, at],
            c,
            peer,
        )

    def window_pass(it, k):
        at = lax.rem(r + k, rows)
        return copy(
            shard_of(windows[it], at),
            shard_of(windows[it], at),
            win_pass.at[it, k],
            win_recv.at[it, at],
            partner,
            r,
        )


    def mix_copy(it):
        return copy(
            mix_out.at[it], mix_in.at[it], mix_send.at[it], mix_recv.at[it], partner, r
        )

    def zone_copy(it, k, arrival=False):
        peer = lax.rem(r + k, rows)
        return copy(
            zone_out.at[it, peer],
            zone_in.at[it, peer if arrival else r],
            zone_send.at[it, k],
            zone_recv.at[it, peer if arrival else r],
            c,
            peer,
        )

    def total_copy(it, col, to):
        return copy(
            total_out.at[it], total_in.at[it, col], total_send.at[it], total_recv.at[it, col], to, r
        )


    def pair_copy(it, k):
        return copy(
            pair_out.at[it, k],
            pair_in.at[it, k],
            pair_send.at[it, k],
            pair_recv.at[it, k],
            partner,
            r,
        )

    def row_copy(it, k):
        peer = peer_chip(k)
        return copy(
            row_out.at[it, peer],
            row_in.at[it, chip],
            row_send.at[it, k],
            row_recv.at[it, chip],
            peer * CORES + core,
            r,
        )

    def row_arrival(it, src):
        return copy(
            row_out.at[it, src],
            row_in.at[it, src],
            row_send.at[it, 0],
            row_recv.at[it, src],
            src * CORES + core,
            r,
        )

    def prepare_volume():
        line = lax.div(surf_ref[r * lines + q], rows)
        for side_of, edge_of_tile in ((0, first_of_tile), (1, last_of_tile)):
            to = pl.ds(0 if side_of == 0 else LANES + shard, LANES)
            at = m * shard - LANES if side_of == 0 else m * shard + shard
            at = pl.multiple_of(jnp.clip(at, 0, nodes - LANES), LANES)
            receives = halo_receives[side_of]

            @pl.when(jnp.logical_not(edge_of_tile))
            def _():
                index_ext[:, to] = index_ref[line, :, pl.ds(at, LANES)]
                source_ext[:, to] = source_ref[line, :, pl.ds(at, LANES)]

            @pl.when(receives)
            def _():
                for kind in range(2):
                    halo_copy(kind, side_of, True).wait_recv()
                index_ext[:, to] = halo_index[side_of, line]
                source_ext[:, to] = halo_source[side_of, line]

            @pl.when(edge_of_tile & jnp.logical_not(receives))
            def _():
                index_ext[:, to] = jnp.full((layers, LANES), levels, I32)
                source_ext[:, to] = jnp.zeros((layers, LANES), F32)

        at = pl.multiple_of(m * shard, LANES)
        index_ext[:, LANES : LANES + shard] = index_ref[line, :, pl.ds(at, shard)]
        source_ext[:, LANES : LANES + shard] = source_ref[line, :, pl.ds(at, shard)]
        indices = index_ext[...]
        coefs = jnp.zeros((layers, span), F32)
        for level in range(levels):
            coefs = jnp.where(indices == level, table_ref[level], coefs)
        coef_ext[...] = coefs
        inside = index_ext[0:1, :] < levels
        for layer in range(layers):
            k = coef_ext[layer : layer + 1, :]
            left = 0.5 * (k + pltpu.roll(k, 1, 1))
            right = 0.5 * (k + pltpu.roll(k, span - 1, 1))
            up = 0.5 * (k + coef_ext[layer - 1 : layer, :]) if layer else k
            diagonal = left + right + up + CELL_MASS
            parts = [left, right, up]
            if layer < layers - 1:
                down = 0.5 * (k + coef_ext[layer + 1 : layer + 2, :])
                diagonal = diagonal + down
                parts.append(down)
            else:
                parts.append(None)
            parts.append(source_ext[layer : layer + 1, :])
            scale = jnp.where(inside, JACOBI_WEIGHT / diagonal, 0.0)
            for kind, part in enumerate(parts):
                if part is not None:
                    weights[kind, layer] = jnp.broadcast_to(part * scale, (SUB, span))

    def relax(now, g, first):
        at = pl.ds(g * SUB, SUB)
        for layer in range(layers):
            value = weights[4, layer]
            if first:
                if layer == 0:
                    value = value + weights[2, layer] * top[at, :]
            else:
                centre = state[now, layer, at, :]
                value = value + (1.0 - JACOBI_WEIGHT) * centre
                value = value + weights[0, layer] * pltpu.roll(centre, 1, 1)
                value = value + weights[1, layer] * pltpu.roll(centre, span - 1, 1)
                above = state[now, layer - 1, at, :] if layer else top[at, :]
                value = value + weights[2, layer] * above
                if layer < layers - 1:
                    value = value + weights[3, layer] * state[now, layer + 1, at, :]
            state[1 - now, layer, at, :] = value

    def volume(it):
        line = lax.div(surf_ref[r * lines + q], rows)
        for side_of, edge_of_tile in ((0, first_of_tile), (1, last_of_tile)):
            dst = (edge_left, edge_right)[side_of]
            to = slice(0, LANES) if side_of == 0 else slice(LANES + shard, span)
            base = row_down if side_of == 0 else row_up
            place = 0
            for z in range(lines):
                place = jnp.where(surf_ref[base * lines + z] == line * rows + base, z, place)
            receives = halo_receives[side_of]

            @pl.when(jnp.logical_not(edge_of_tile))
            def _():
                edge_near(it, side_of, True).wait_recv()
                top[:, to] = dst[it, lines].astype(F32)

            @pl.when(receives)
            def _():
                for z in range(lines):
                    edge_far_arrival(it, side_of, z).wait_recv()
                value = dst[it, 0]
                for z in range(1, lines):
                    value = jnp.where(place == z, dst[it, z], value)
                top[:, to] = value.astype(F32)

            @pl.when(edge_of_tile & jnp.logical_not(receives))
            def _():
                top[:, to] = jnp.zeros((rhs, LANES), F32)

        def rows_of(g, _):
            for i in range(SWEEPS):
                relax(i % 2, g, it == 0 and i == 0)
            at = pl.ds(g * SUB, SUB)
            k = jnp.broadcast_to(coef_ext[0:1, LANES : LANES + shard], (SUB, shard))
            flux[at, :] = k * (
                top[at, LANES : LANES + shard]
                - state[SWEEPS % 2, 0, at, LANES : LANES + shard]
            )
            return 0

        lax.fori_loop(0, rhs // SUB, rows_of, 0)

    def segments(which, traces_of, contract):
        def step(k, acc):
            s = order[4 * which, k]
            keep = order[4 * which + 2, k].astype(F32)
            acc = acc * keep + lax.dot_general(
                traces_of[order[4 * which + 1, k]],
                panel[s],
                (((1,), (contract,)), ((), ())),
                preferred_element_type=F32,
            )
            product[k] = acc
            return acc

        acc = jnp.zeros((rhs, tile), F32)
        for k in range(slots):
            acc = step(k, acc)

    def last_of(which, at):
        return product[order[4 * which + 3, at]]

    def dense_part(it):
        @pl.when(is_dense & (core == 0) & (c == 0))
        def _():
            for k in range(1, rows):
                window_copy(it, k).start()

        for k in range(1, chips):
            band_copy(it, k, True).wait_recv()
            band_pass(it, k).start()

            @pl.when((core == 0) & (peer_chip(k) == 0))
            def _():
                for j in range(1, rows):
                    window_copy(it, j).start()

        for k in range(chips):
            band_pass(it, k, True).wait_recv()
        windows[it][pl.ds(r * per_shard, per_shard)] = bands[it][0:per_shard]
        if it == 0:
            pltpu.make_async_copy(tab, order, tab_sem).wait()

            def landed(s, _):
                panel_copy(s).wait()
                return 0

            lax.fori_loop(0, slots, landed, 0)

        segments(0, bands[it], 0)
        for z in range(rows):
            for p in range(half):
                value = last_of(0, z * per_shard + other * half + p)
                mix_out[it, z, p] = value.astype(BF16)
        mix_copy(it).start()

        @pl.when(core == 0)
        def _():
            for k in range(1, rows):
                window_copy(it, k, True).wait_recv()
                window_pass(it, k).start()

        mix_copy(it).wait_recv()
        for z in range(rows):
            for p in range(half):
                value = last_of(0, z * per_shard + core * half + p) + mix_in[it, z, p].astype(F32)
                zone_out[it, z, p] = value.astype(BF16)
        for p in range(half):
            zone_own[p] = last_of(0, r * per_shard + core * half + p) + mix_in[it, r, p].astype(F32)
        for k in range(1, rows):
            zone_copy(it, k).start()

        @pl.when(core == 1)
        def _():
            for k in range(1, rows):
                window_copy(it, k, True).wait_recv()

        segments(1, windows[it], 1)
        for k in range(chips):
            for p in range(per_shard):
                value = last_of(1, (k * CORES + other) * per_shard + p)
                pair_out[it, k, p] = value.astype(BF16)
            pair_copy(it, k).start()
        for k in range(chips):
            pair_copy(it, k).wait_recv()
        for k in range(1, chips):
            peer = peer_chip(k)
            for p in range(per_shard):
                value = last_of(1, (peer * CORES + core) * per_shard + p)
                value = value + pair_in[it, peer, p].astype(F32)
                row_out[it, peer, p] = value.astype(BF16)
            row_copy(it, k).start()
        for p in range(per_shard):
            row_own[p] = last_of(1, c * per_shard + p) + pair_in[it, chip, p].astype(F32)
        for k in range(1, rows):
            zone_copy(it, k, True).wait_recv()
        for p in range(half):
            value = zone_own[p]
            for k in range(1, rows):
                value = value + zone_in[it, lax.rem(r + k, rows), p].astype(F32)
            zone_own[p] = value
            total_out[it, p] = value.astype(BF16)

        @pl.when(c != 0)
        def _():
            total_copy(it, c, 0).start()

    for it in range(ITERS):
        for p in range(per_shard):
            rounded = traces_ref[:, p * tile : (p + 1) * tile].astype(BF16)
            bands[it][c * per_shard + p] = rounded
            top[:, LANES + p * tile : LANES + (p + 1) * tile] = rounded.astype(F32)

        @pl.when(jnp.logical_not(last_of_tile))
        def _():
            edge_near(it, 0).start()

        @pl.when(jnp.logical_not(first_of_tile))
        def _():
            edge_near(it, 1).start()

        @pl.when(cross_right)
        def _():
            for z in range(lines):
                edge_far(it, 0, z).start()

        @pl.when(cross_left)
        def _():
            for z in range(lines):
                edge_far(it, 1, z).start()

        if it == 0:
            for side_of in range(2):

                @pl.when(halo_sends[side_of])
                def _():
                    for kind in range(2):
                        halo_copy(kind, side_of).start()

        for k in range(1, chips):

            @pl.when(peer_chip(k) < dense_chips)
            def _():
                band_copy(it, k).start()

        @pl.when(is_dense)
        def _():
            band_pass(it, 0).start()

        if it == 0:
            prepare_volume()
        volume(it)

        @pl.when(is_dense)
        def _():
            dense_part(it)

        if it == 0:
            input_copy(3).wait()

        response_ref[...] = flux[...]
        for src in range(dense_chips):

            @pl.when(src != chip)
            def _():
                row_arrival(it, src).wait_recv()
                for p in range(per_shard):
                    at = slice(p * tile, (p + 1) * tile)
                    response_ref[:, at] += row_in[it, src, p].astype(F32)

        @pl.when(is_dense)
        def _():
            for p in range(per_shard):
                at = slice(p * tile, (p + 1) * tile)
                response_ref[:, at] += row_own[p]

        @pl.when(c == 0)
        def _():
            for p in range(half):
                at = slice(p * tile, (p + 1) * tile)
                response_ref[:, at] += zone_own[p]
            for src in range(1, dense):
                total_copy(it, src, src).wait_recv()
                for p in range(half):
                    at = (src % CORES) * half + p
                    at = slice(at * tile, (at + 1) * tile)
                    response_ref[:, at] += total_in[it, src, p].astype(F32)

        t = traces_ref[...]
        traces_ref[...] = t + COUPLING_STEP * (load_ref[...] - t - response_ref[...])

    for it in range(ITERS):

        @pl.when(jnp.logical_not(last_of_tile))
        def _():
            edge_near(it, 0).wait_send()

        @pl.when(jnp.logical_not(first_of_tile))
        def _():
            edge_near(it, 1).wait_send()

        @pl.when(cross_right)
        def _():
            for z in range(lines):
                edge_far(it, 0, z).wait_send()

        @pl.when(cross_left)
        def _():
            for z in range(lines):
                edge_far(it, 1, z).wait_send()

        if it == 0:
            for side_of in range(2):

                @pl.when(halo_sends[side_of])
                def _():
                    for kind in range(2):
                        halo_copy(kind, side_of).wait_send()

        for k in range(1, chips):

            @pl.when(peer_chip(k) < dense_chips)
            def _():
                band_copy(it, k).wait_send()

        @pl.when(is_dense)
        def _():
            for k in range(chips):
                band_pass(it, k).wait_send()
                pair_copy(it, k).wait_send()
            for k in range(1, chips):
                row_copy(it, k).wait_send()
            mix_copy(it).wait_send()
            for k in range(1, rows):
                zone_copy(it, k).wait_send()

            @pl.when(core == 0)
            def _():
                for k in range(1, rows):
                    window_copy(it, k).wait_send()
                    window_pass(it, k).wait_send()

            @pl.when(c != 0)
            def _():
                total_copy(it, c, 0).wait_send()


def local(
    trace_start, surface_load, panel_tiles, tile_list, surf_map, coef_index, coef_table, vol_source
):
    cols = lax.axis_size("col")
    rows = lax.axis_size("row")
    lines, layers, nodes = coef_index.shape
    slots, tile, _ = panel_tiles.shape
    rhs, shard = trace_start.shape
    per_shard = shard // tile
    levels = coef_table.shape[0]
    half = per_shard // CORES
    chips = cols // CORES
    span = shard + 2 * LANES
    cfg = (cols, rows, lines, per_shard, tile, slots, nodes, layers, rhs, levels)
    smem = pl.BlockSpec(memory_space=pltpu.SMEM)
    vmem = pl.BlockSpec(memory_space=pltpu.VMEM)
    hbm = pl.BlockSpec(memory_space=pl.ANY)
    block = (rhs, tile)
    dma = pltpu.SemaphoreType.DMA
    out = jax.ShapeDtypeStruct((rhs, shard), F32)
    return pl.pallas_call(
        functools.partial(kernel, cfg),
        out_shape=(out, out),
        in_specs=[smem] * 3 + [hbm] * 5,
        out_specs=(vmem, vmem),
        scratch_shapes=[
            pltpu.VMEM((slots, tile, tile), BF16),
            pltpu.VMEM((rhs, shard), F32),
            pltpu.VMEM((lines, layers, nodes), I32),
            pltpu.VMEM((lines, layers, nodes), F32),
            pltpu.VMEM((SUB, LANES), I32),
            pltpu.SMEM((SUB, LANES), I32),
            pltpu.VMEM((cols * per_shard,) + block, BF16),
            pltpu.VMEM((cols * per_shard,) + block, BF16),
            pltpu.VMEM((rows * per_shard,) + block, BF16),
            pltpu.VMEM((rows * per_shard,) + block, BF16),
            pltpu.VMEM((ITERS, lines + 1, rhs, LANES), BF16),
            pltpu.VMEM((ITERS, lines + 1, rhs, LANES), BF16),
            pltpu.VMEM((2, lines, layers, LANES), I32),
            pltpu.VMEM((2, lines, layers, LANES), F32),
            pltpu.VMEM((slots + 1,) + block, F32),
            pltpu.VMEM((ITERS, rows, half) + block, BF16),
            pltpu.VMEM((ITERS, rows, half) + block, BF16),
            pltpu.VMEM((half,) + block, F32),
            pltpu.VMEM((ITERS, rows, half) + block, BF16),
            pltpu.VMEM((ITERS, rows, half) + block, BF16),
            pltpu.VMEM((ITERS, half) + block, BF16),
            pltpu.VMEM((ITERS, cols, half) + block, BF16),
            pltpu.VMEM((ITERS, chips, per_shard) + block, BF16),
            pltpu.VMEM((ITERS, chips, per_shard) + block, BF16),
            pltpu.VMEM((per_shard,) + block, F32),
            pltpu.VMEM((ITERS, chips, per_shard) + block, BF16),
            pltpu.VMEM((ITERS, chips, per_shard) + block, BF16),
            pltpu.VMEM((layers, span), I32),
            pltpu.VMEM((layers, span), F32),
            pltpu.VMEM((layers, span), F32),
            pltpu.VMEM((5, layers, SUB, span), F32),
            pltpu.VMEM((2, layers, rhs, span), F32),
            pltpu.VMEM((rhs, span), F32),
            pltpu.VMEM((rhs, shard), F32),
            dma((slots,)),
            dma((4,)),
            dma,
            dma((ITERS, chips)),
            dma((ITERS, chips)),
            dma((ITERS, cols)),
            dma((ITERS, rows)),
            dma((ITERS, rows)),
            dma((ITERS, rows)),
            dma((ITERS, 2, lines + 1)),
            dma((ITERS, 2, lines + 1)),
            dma((2, 2)),
            dma((2, 2)),
            dma((ITERS,)),
            dma((ITERS,)),
            dma((ITERS, rows)),
            dma((ITERS, rows)),
            dma((ITERS,)),
            dma((ITERS, cols)),
            dma((ITERS, chips)),
            dma((ITERS, chips)),
            dma((ITERS, chips)),
            dma((ITERS, chips)),
        ],
        compiler_params=pltpu.CompilerParams(
            collective_id=0, has_side_effects=True, vmem_limit_bytes=60 * 1024 * 1024
        ),
        name="coupled",
    )(
        tile_list,
        surf_map,
        coef_table,
        trace_start,
        surface_load,
        coef_index,
        vol_source,
        panel_tiles,
    )


def solution(mesh):
    return jax.shard_map(
        local,
        mesh=mesh,
        in_specs=(
            P(None, ("col", "row")),
            P(None, ("col", "row")),
            P(("col", "row"), None, None),
            P(("col", "row")),
            P(),
            P(None, None, "row"),
            P(),
            P(None, None, "row"),
        ),
        out_specs=(P(None, ("col", "row")), P(None, ("col", "row"))),
        check_vma=False,
    )
```

time: 86.4 us -> 51.8 us (0.60)
  Pallas kernels: 79.7 us -> 47.8 us
  other arithmetic: 2.6 us -> 0 us
    pallas_call x1, Pallas kernels: 79.7 us -> 47.8 us  [local(): pl.pallas_call(functools.partial(kernel, cfg), out_shape=(out, out), in_s...]
    select_n x1 -> x0, other arithmetic: 1.19 us -> none  [local(): col_tile = safe % side]
where the time goes in v1:
time: 51.8 us; the launch traced here: 51.6 us
  Pallas kernels  47.8 us (92%)
  local copies, waits for them, and re-layouts  3.14 us (6%)
  between operations  0.64 us (1%)
    pallas_call x1, Pallas kernels, local(): pl.pallas_call(functools.partial(kernel, cfg), out_shape=(out, out), in_s...  47.8 us
    unnamed x2, local copies, waits for them, and re-layouts  3.14 us

profile of v1, /device:TPU:0, one launch (start us, length us, event | category | flops | bytes accessed | tf_op | source)
XLA Modules:
  0.0 51.6 jit_solution(16343608058658976509)
XLA Ops:
  0.6 47.8 %coupled.1 = (f32[32,1024]{1,0:T(8,128)}, f32[32,1024]{1,0:T(8,128)}) custom-call(s32[22]{0:T(128)} %list_ref.1, s32[8]{0:T(128)} %surf_ref.1, f32[16]{0:T(128)} %table_ref.1, f32[32,1024]{1,0:T(8,128)} %start_hbm.1, f32[32,1024]{1,0:T(8,128)} %load_hbm.1, s32[2,4,4096]{2,1,0:T(4,128)} %index_hbm.1, f32[2,4,4096]{2,1,0:T(4,128)} %source_hbm.1, ...), custom_call_target="tpu_custom_call" | custom-call | tf_op jit(solution)/shard_map/coupled/pallas_call | solution.py:796
  48.5 1.6 %copy.12 = f32[32,1024]{1,0:T(8,128)} copy(f32[32,1024]{1,0:T(8,128)} %get-tuple-element.4) | data formatting | bytes 262144
  50.0 1.6 %copy.13 = f32[32,1024]{1,0:T(8,128)} copy(f32[32,1024]{1,0:T(8,128)} %get-tuple-element.5) | data formatting | bytes 262144

commit v2 on v1

v2 whole, which is shorter than its diff:
```python
import functools

import jax
import jax.numpy as jnp
from jax import lax
from jax.experimental import pallas as pl
from jax.experimental.pallas import tpu as pltpu
from jax.sharding import PartitionSpec as P

ITERS = 2
SWEEPS = 4

COUPLING_STEP = 0.3
JACOBI_WEIGHT = 0.8
CELL_MASS = 0.05

LANES = 128
SUB = 8
CORES = 2
TURNED_BYTES = 36 * 1024 * 1024
F32 = jnp.float32
BF16 = jnp.bfloat16
I32 = jnp.int32


def quotient(x, n):
    return x >> (n.bit_length() - 1) if n & (n - 1) == 0 else lax.div(x, n)


def remainder(x, n):
    return x & (n - 1) if n & (n - 1) == 0 else lax.rem(x, n)


def kernel(
    cfg,
    list_hbm,
    surf_hbm,
    table_hbm,
    start_hbm,
    load_hbm,
    index_hbm,
    source_hbm,
    panel_hbm,
    middle_hbm,
    product_hbm,
    flux_hbm,
    middle_ref,
    product_ref,
    flux,
    list_ref,
    surf_ref,
    table_ref,
    panel,
    turned,
    traces_ref,
    load_ref,
    index_ref,
    source_ref,
    tab,
    order,
    near_band0,
    near_band1,
    far_band0,
    far_band1,
    near_window0,
    near_window1,
    far_window0,
    far_window1,
    edge_out,
    edge_left,
    edge_right,
    halo_index,
    halo_source,
    product,
    mix_out,
    mix_in,
    zone_own,
    zone_out,
    zone_in,
    total_own,
    total_out,
    total_in,
    pair_out,
    pair_in,
    row_own,
    row_out,
    row_in,
    index_ext,
    coef_ext,
    source_ext,
    weights,
    state,
    top,
    panel_sem,
    input_sem,
    output_sem,
    tab_sem,
    band_send,
    pass_send,
    near_recv,
    far_recv,
    win_send,
    win_pass,
    win_recv,
    win_far,
    edge_send,
    edge_recv,
    halo_send,
    halo_recv,
    mix_send,
    mix_recv,
    zone_send,
    zone_recv,
    total_send,
    total_recv,
    pair_send,
    pair_recv,
    row_send,
    row_recv,
):
    cols, rows, lines, per_shard, tile, slots, nodes, layers, rhs, levels, turns = cfg
    dense = cols - lines
    group = cols // lines
    shard = per_shard * tile
    half = per_shard // CORES
    chips = cols // CORES
    dense_chips = dense // CORES
    win_tiles = rows * per_shard
    band_tiles = cols * per_shard
    side = cols * rows * per_shard
    span = shard + 2 * LANES
    wide = tile // 2
    near_bands = (near_band0, near_band1)
    far_bands = (far_band0, far_band1)
    near_windows = (near_window0, near_window1)
    far_windows = (far_window0, far_window1)
    c = lax.axis_index("col")
    r = lax.axis_index("row")
    core = lax.rem(c, CORES)
    chip = lax.div(c, CORES)
    other = 1 - core
    partner = chip * CORES + other
    q = lax.div(c, group)
    m = lax.rem(c, group)
    is_dense = c < dense
    row_up = jnp.minimum(r + 1, rows - 1)
    row_down = jnp.maximum(r - 1, 0)
    first_of_tile = m == 0
    last_of_tile = m == group - 1
    cross_left = first_of_tile & (r > 0)
    cross_right = last_of_tile & (r < rows - 1)

    def copy(src, dst, send, recv, to_col, to_row):
        return pltpu.make_async_remote_copy(
            src_ref=src,
            dst_ref=dst,
            send_sem=send,
            recv_sem=recv,
            device_id=(to_col, to_row),
            device_id_type=pl.DeviceIdType.MESH,
        )

    stops = sorted({0, slots // 4, slots // 2 // 2 * 2, slots})

    def panel_copy(i):
        part = pl.ds(stops[i], stops[i + 1] - stops[i])
        return pltpu.make_async_copy(panel_hbm.at[part], panel.at[part], panel_sem.at[i])

    inputs = (
        (start_hbm, traces_ref),
        (index_hbm, index_ref),
        (source_hbm, source_ref),
        (load_hbm, load_ref),
        (list_hbm, list_ref),
        (surf_hbm, surf_ref),
        (table_hbm, table_ref),
    )

    def input_copy(i):
        return pltpu.make_async_copy(inputs[i][0], inputs[i][1], input_sem.at[i])

    outputs = ((middle_ref, middle_hbm), (product_ref, product_hbm), (flux, flux_hbm))

    def output_copy(i):
        return pltpu.make_async_copy(outputs[i][0], outputs[i][1], output_sem.at[i])

    barrier = pltpu.get_barrier_semaphore()

    def greet(to_col, to_row):
        pl.semaphore_signal(
            barrier, inc=1, device_id=(to_col, to_row), device_id_type=pl.DeviceIdType.MESH
        )

    for k in range(1, rows):
        greet(c, lax.rem(r + k, rows))
    for k in range(1, cols):
        greet(lax.rem(c + k, cols), r)

    @pl.when(cross_right)
    def _():
        for z in range(lines):
            greet(z * group, row_up)

    @pl.when(cross_left)
    def _():
        for z in range(lines):
            greet(z * group + group - 1, row_down)

    for i in (4, 0, 1, 2, 5, 6, 3):
        input_copy(i).start()

    @pl.when(is_dense)
    def _():
        for i in range(len(stops) - 1):
            panel_copy(i).start()


    padded_slots = -(-slots // SUB) * SUB
    lane = lax.broadcasted_iota(I32, (SUB, LANES), 1)

    def sort_slots():
        slot = lax.broadcasted_iota(I32, (padded_slots, LANES), 0)
        lanes = lax.broadcasted_iota(I32, (padded_slots, LANES), 1)
        row_key = jnp.full((padded_slots, LANES), band_tiles, I32)
        col_key = jnp.full((padded_slots, LANES), win_tiles, I32)
        keys = []
        for s in range(slots):
            name = list_ref[s]
            safe = jnp.maximum(name, 0)
            row = quotient(safe, side)
            row = quotient(quotient(row, per_shard), rows) * per_shard + remainder(row, per_shard)
            row = jnp.where(name >= 0, row, band_tiles)
            col = jnp.where(name >= 0, remainder(safe, side), win_tiles)
            keys.append((col, row))
            row_key = jnp.where(slot == s, row, row_key)
            col_key = jnp.where(slot == s, col, col_key)

        def fold(x):
            x = functools.reduce(jnp.add, [x[i : i + SUB] for i in range(0, padded_slots, SUB)])
            for shift in (4, 2, 1):
                x = x + pltpu.roll(x, shift, 0)
            return x

        for which, key, source, count in (
            (0, col_key, row_key, win_tiles),
            (1, row_key, col_key, band_tiles),
        ):
            rank = jnp.zeros((padded_slots, LANES), I32)
            upto = jnp.zeros((SUB, LANES), I32)
            equal = jnp.zeros((SUB, LANES), I32)
            for s in range(slots):
                value = keys[s][which]
                ahead = (key > value) | ((key == value) & (slot > s))
                rank = rank + jnp.where(ahead, 1, 0)
                upto = upto + jnp.where(lane >= value, 1, 0)
                equal = equal + jnp.where(lane == value, 1, 0)
            rank = jnp.where(slot < slots, rank, LANES)
            here = rank == lanes
            place = fold(jnp.where(here, slot, 0))
            origin = fold(jnp.where(here, jnp.where(key < count, source, 0), 0))
            value = fold(jnp.where(here, key, 0))
            keep = (value == pltpu.roll(value, 1, 1)) & (lane > 0)
            last = jnp.where(equal > 0, upto - 1, slots)
            for i, x in enumerate((place, origin, jnp.where(keep, 1, 0), last)):
                tab[4 * which + i : 4 * which + i + 1, :] = x[0:1, :]

    input_copy(4).wait()

    @pl.when(is_dense)
    def _():
        sort_slots()
        pltpu.make_async_copy(tab, order, tab_sem).start()
        product[slots] = jnp.zeros((rhs, tile), F32)

    input_copy(0).wait()
    input_copy(1).wait()
    input_copy(2).wait()
    input_copy(5).wait()
    input_copy(6).wait()

    expected = (
        cols - 1 + rows - 1 + jnp.where(cross_right, lines, 0) + jnp.where(cross_left, lines, 0)
    )
    pl.semaphore_wait(barrier, expected)

    def settle(ref, sem):
        copy(ref, ref, sem, sem, partner, r).wait_recv()

    def settle_send(ref, sem):
        copy(ref, ref, sem, sem, partner, r).wait_send()


    def halo_copy(kind, side_of, arrival=False):
        ref = (index_ref, source_ref)[kind]
        dst = (halo_index, halo_source)[kind]
        at = nodes - LANES if side_of == 0 else 0
        to = row_up if (side_of == 0) != arrival else row_down
        return copy(
            ref.at[:, :, pl.ds(at, LANES)],
            dst.at[side_of],
            halo_send.at[side_of],
            halo_recv.at[side_of],
            c,
            to,
        )

    halo_sends = (first_of_tile & (r < rows - 1), last_of_tile & (r > 0))
    halo_receives = (cross_left, cross_right)


    def edge_near(it, side_of):
        dst = (edge_left, edge_right)[side_of]
        return copy(
            edge_out.at[it, side_of],
            dst.at[it, lines],
            edge_send.at[it, side_of],
            edge_recv.at[it, side_of],
            c + 1 if side_of == 0 else c - 1,
            r,
        )

    def edge_far(it, side_of, z):
        dst = (edge_left, edge_right)[side_of]
        to = (z * group, row_up) if side_of == 0 else (z * group + group - 1, row_down)
        return copy(
            edge_out.at[it, side_of],
            dst.at[it, q],
            edge_send.at[it, side_of],
            edge_recv.at[it, side_of],
            *to,
        )


    def shards(ref, col, count=1):
        return ref.at[pl.ds(col * per_shard, count * per_shard)]

    bits = chips.bit_length() - 1
    power = chips == 1 << bits
    near_first = sorted(range(1, chips), key=lambda k: k.bit_count() if power else k)
    far_first = near_first[::-1]

    def peer_chip(k):
        if not power:
            return lax.rem(chip + k, chips)
        digits = [remainder(quotient(chip, 1 << b), 2) for b in range(bits)]
        return sum((1 - d if k >> b & 1 else d) * (1 << b) for b, d in enumerate(digits))

    def band_copies(it, k):
        peer = peer_chip(k) * CORES
        send, recv = band_send.at[it], near_recv.at[it, chip]
        near, far = shards(near_bands[it], c), shards(far_bands[it], c)
        return copy(near, near, send, recv, peer + core, r), copy(far, near, send, recv, peer + other, r)

    def partner_copies(it):
        near, far = shards(near_bands[it], c), shards(far_bands[it], c)
        return (
            copy(far, near, band_send.at[it], near_recv.at[it, chip], partner, r),
            copy(near, far, pass_send.at[it], far_recv.at[it], partner, r),
        )

    def band_pass(it, k):
        at = peer_chip(k) * CORES
        return copy(
            shards(near_bands[it], at, CORES),
            shards(far_bands[it], at, CORES),
            pass_send.at[it],
            far_recv.at[it],
            partner,
            r,
        )

    def to_rows(send):
        for d in range(rows - 1, 0, -1):

            @pl.when(r + d < rows)
            def _():
                send(r + d)

            @pl.when(r >= d)
            def _():
                send(r - d)

    def window_copy(it, peer):
        return copy(
            shards(near_bands[it], 0),
            shards(near_windows[it], r),
            win_send.at[it],
            win_recv.at[it, r],
            c,
            peer,
        )

    def window_pass(it, at):
        return copy(
            shards(near_windows[it], at),
            shards(far_windows[it], at),
            win_pass.at[it],
            win_far.at[it],
            partner,
            r,
        )

    def send_window(it):
        to_rows(lambda peer: window_copy(it, peer).start())


    def mix_copy(it, h):
        return copy(
            mix_out.at[it, h], mix_in.at[it, h], mix_send.at[it], mix_recv.at[it, h], partner, r
        )

    def zone_copy(it, h, peer):
        return copy(
            zone_out.at[it, h, peer],
            zone_in.at[it, h, r],
            zone_send.at[it],
            zone_recv.at[it],
            c,
            peer,
        )

    def total_copy(it):
        return copy(
            total_out.at[it], total_in.at[it, c], total_send.at[it], total_recv.at[it], 0, r
        )


    def pair_copy(it, h):
        return copy(
            pair_out.at[it, h],
            pair_in.at[it, h],
            pair_send.at[it],
            pair_recv.at[it, h],
            partner,
            r,
        )

    def row_copy(it, h, k):
        peer = peer_chip(k)
        return copy(
            row_out.at[it, h, peer],
            row_in.at[it, h, chip],
            row_send.at[it],
            row_recv.at[it],
            peer * CORES + core,
            r,
        )

    def prepare_volume():
        line = lax.div(surf_ref[r * lines + q], rows)
        for side_of, edge_of_tile in ((0, first_of_tile), (1, last_of_tile)):
            to = pl.ds(0 if side_of == 0 else LANES + shard, LANES)
            at = m * shard - LANES if side_of == 0 else m * shard + shard
            at = pl.multiple_of(jnp.clip(at, 0, nodes - LANES), LANES)
            receives = halo_receives[side_of]

            @pl.when(jnp.logical_not(edge_of_tile))
            def _():
                index_ext[:, to] = index_ref[line, :, pl.ds(at, LANES)]
                source_ext[:, to] = source_ref[line, :, pl.ds(at, LANES)]

            @pl.when(receives)
            def _():
                settle(halo_source, halo_recv.at[side_of])
                index_ext[:, to] = halo_index[side_of, line]
                source_ext[:, to] = halo_source[side_of, line]

            @pl.when(edge_of_tile & jnp.logical_not(receives))
            def _():
                index_ext[:, to] = jnp.full((layers, LANES), levels, I32)
                source_ext[:, to] = jnp.zeros((layers, LANES), F32)

        at = pl.multiple_of(m * shard, LANES)
        index_ext[:, LANES : LANES + shard] = index_ref[line, :, pl.ds(at, shard)]
        source_ext[:, LANES : LANES + shard] = source_ref[line, :, pl.ds(at, shard)]
        indices = index_ext[...]
        coefs = jnp.zeros((layers, span), F32)
        for level in range(levels):
            coefs = jnp.where(indices == level, table_ref[level], coefs)
        coef_ext[...] = coefs
        inside = index_ext[0:1, :] < levels
        for layer in range(layers):
            k = coef_ext[layer : layer + 1, :]
            left = 0.5 * (k + pltpu.roll(k, 1, 1))
            right = 0.5 * (k + pltpu.roll(k, span - 1, 1))
            up = 0.5 * (k + coef_ext[layer - 1 : layer, :]) if layer else k
            diagonal = left + right + up + CELL_MASS
            parts = [left, right, up]
            if layer < layers - 1:
                down = 0.5 * (k + coef_ext[layer + 1 : layer + 2, :])
                diagonal = diagonal + down
                parts.append(down)
            else:
                parts.append(None)
            parts.append(source_ext[layer : layer + 1, :])
            scale = jnp.where(inside, JACOBI_WEIGHT / diagonal, 0.0)
            for kind, part in enumerate(parts):
                if part is not None:
                    weights[kind, layer] = jnp.broadcast_to(part * scale, (SUB, span))

    def relax(now, g, first):
        at = pl.ds(g * SUB, SUB)
        for layer in range(layers):
            value = weights[4, layer]
            if first:
                if layer == 0:
                    value = value + weights[2, layer] * top[at, :]
            else:
                centre = state[now, layer, at, :]
                value = value + (1.0 - JACOBI_WEIGHT) * centre
                value = value + weights[0, layer] * pltpu.roll(centre, 1, 1)
                value = value + weights[1, layer] * pltpu.roll(centre, span - 1, 1)
                above = state[now, layer - 1, at, :] if layer else top[at, :]
                value = value + weights[2, layer] * above
                if layer < layers - 1:
                    value = value + weights[3, layer] * state[now, layer + 1, at, :]
            state[1 - now, layer, at, :] = value

    def gather_top(it):
        line = lax.div(surf_ref[r * lines + q], rows)
        for side_of, edge_of_tile in ((0, first_of_tile), (1, last_of_tile)):
            dst = (edge_left, edge_right)[side_of]
            to = slice(0, LANES) if side_of == 0 else slice(LANES + shard, span)
            base = row_down if side_of == 0 else row_up
            place = 0
            for z in range(lines):
                place = jnp.where(surf_ref[base * lines + z] == line * rows + base, z, place)
            receives = halo_receives[side_of]

            @pl.when(jnp.logical_not(edge_of_tile))
            def _():
                settle(dst.at[it, lines], edge_recv.at[it, side_of])
                top[:, to] = dst[it, lines].astype(F32)

            @pl.when(receives)
            def _():
                settle(dst.at[it, pl.ds(0, lines)], edge_recv.at[it, side_of])
                value = dst[it, 0]
                for z in range(1, lines):
                    value = jnp.where(place == z, dst[it, z], value)
                top[:, to] = value.astype(F32)

            @pl.when(edge_of_tile & jnp.logical_not(receives))
            def _():
                top[:, to] = jnp.zeros((rhs, LANES), F32)

    def relax_groups(it, begin, end):
        def rows_of(g, _):
            for i in range(SWEEPS):
                relax(i % 2, g, it == 0 and i == 0)
            at = pl.ds(g * SUB, SUB)
            k = jnp.broadcast_to(coef_ext[0:1, LANES : LANES + shard], (SUB, shard))
            flux[at, :] = k * (
                top[at, LANES : LANES + shard]
                - state[SWEEPS % 2, 0, at, LANES : LANES + shard]
            )
            return 0

        lax.fori_loop(begin, end, rows_of, 0)

    def lanes_of(h):
        return slice(h * wide, (h + 1) * wide)

    def segments(which, traces_of, part, h=None):
        at = slice(None) if h is None else lanes_of(h)
        part = pl.ds(pl.multiple_of(part * wide, wide), wide)
        acc = jnp.zeros((rhs, tile if h is None else wide), F32)
        for k in range(slots):
            s = order[4 * which, k]
            traces = traces_of[order[4 * which + 1, k]]
            keep = order[4 * which + 2, k].astype(F32)
            if which == 0:
                term = jnp.dot(traces, panel[s, part, at], preferred_element_type=F32)
            elif turns == slots or k < turns:
                block = turned[s if turns == slots else k, part, at]
                term = jnp.dot(traces, block, preferred_element_type=F32)
            else:
                block = panel[s, at, part]
                contract = (((1,), (1,)), ((), ()))
                term = lax.dot_general(traces, block, contract, preferred_element_type=F32)
            acc = acc * keep + term
            product[k, :, at] = acc if h is None else product[k, :, at] + acc

    def last_of(which, h, at):
        return product[order[4 * which + 3, at], :, lanes_of(h)]

    def send_mix(it, h):
        for z in range(rows):
            for p in range(half):
                value = last_of(0, h, z * per_shard + other * half + p)
                mix_out[it, h, z, p] = value.astype(BF16)
                zone_own[h, z, p] = last_of(0, h, z * per_shard + core * half + p)
        mix_copy(it, h).start()

    def send_zone(it, h):
        settle(mix_in.at[it, h], mix_recv.at[it, h])
        for z in range(rows):
            for p in range(half):
                value = zone_own[h, z, p] + mix_in[it, h, z, p].astype(F32)
                zone_own[h, z, p] = value
                zone_out[it, h, z, p] = value.astype(BF16)
        to_rows(lambda peer: zone_copy(it, h, peer).start())

    def send_pair(it, h):
        for k in range(chips):
            for p in range(per_shard):
                value = last_of(1, h, (k * CORES + other) * per_shard + p)
                pair_out[it, h, k, p] = value.astype(BF16)
                row_own[h, k, p] = last_of(1, h, (k * CORES + core) * per_shard + p)
        pair_copy(it, h).start()

    def send_rows(it, h):
        settle(pair_in.at[it, h], pair_recv.at[it, h])
        for k in range(chips):
            for p in range(per_shard):
                value = row_own[h, k, p] + pair_in[it, h, k, p].astype(F32)
                row_own[h, k, p] = value
                row_out[it, h, k, p] = value.astype(BF16)
        for k in far_first:
            row_copy(it, h, k).start()

    def wait_panel():
        for i in range(len(stops) - 1):
            panel_copy(i).wait()


    def turn(i):
        begin, end = min(stops[i], turns), min(stops[i + 1], turns)
        if turns == slots:
            panel_copy(i).wait()

        def one(k):
            turned[k] = panel[k if turns == slots else order[4, k]].T

        def two(j, _):
            one(begin + 2 * j)
            one(begin + 2 * j + 1)
            return 0

        lax.fori_loop(0, (end - begin) // 2, two, 0)
        if (end - begin) % 2:
            one(end - 1)

    def dense_part(it):
        near_band, far_band = near_bands[it], far_bands[it]
        near_window, far_window = near_windows[it], far_windows[it]
        if it == 0:
            if turns < slots:
                pltpu.make_async_copy(tab, order, tab_sem).wait()
                wait_panel()
            for i in range(len(stops) - 2):
                turn(i)
        settle(shards(near_band, partner), near_recv.at[it, chip])

        @pl.when(c == 1)
        def _():
            send_window(it)

        for i, k in enumerate(near_first):
            settle(shards(near_band, peer_chip(k) * CORES, CORES), near_recv.at[it, peer_chip(k)])
            band_pass(it, k).start()

            @pl.when(peer_chip(k) == 0)
            def _():
                send_window(it)

            if it == 0 and i == min(1, len(near_first) - 1):
                turn(len(stops) - 2)

        if it == 0 and turns == slots:
            pltpu.make_async_copy(tab, order, tab_sem).wait()
        segments(0, near_band, core)
        settle(shards(far_band, 0, cols - 1), far_recv.at[it])
        near_window[pl.ds(r * per_shard, per_shard)] = near_band[0:per_shard]
        far_window[pl.ds(r * per_shard, per_shard)] = far_band[0:per_shard]
        segments(0, far_band, other, 0)
        send_mix(it, 0)
        segments(0, far_band, other, 1)
        send_mix(it, 1)
        send_zone(it, 0)
        send_zone(it, 1)
        for k in range(1, rows):
            at = lax.rem(r + k, rows)
            settle(shards(near_window, at), win_recv.at[it, at])
            window_pass(it, at).start()
        segments(1, near_window, core)
        settle(shards(far_window, 0, rows - 1), win_far.at[it])
        segments(1, far_window, other, 0)
        send_pair(it, 0)
        segments(1, far_window, other, 1)
        send_pair(it, 1)
        groups = rhs // SUB
        gather_top(it)
        relax_groups(it, 0, groups // 4)
        send_rows(it, 0)
        relax_groups(it, groups // 4, groups // 2)
        send_rows(it, 1)
        settle(zone_in.at[it, :, pl.ds(0, rows - 1)], zone_recv.at[it])
        for p in range(half):
            for h in range(2):
                value = zone_own[h, r, p]
                for k in range(1, rows):
                    value = value + zone_in[it, h, lax.rem(r + k, rows), p].astype(F32)
                total_own[p, :, lanes_of(h)] = value
                total_out[it, p, :, lanes_of(h)] = value.astype(BF16)

        @pl.when(c != 0)
        def _():
            total_copy(it).start()

        relax_groups(it, groups // 2, groups)

    def drain(it):
        for side_of, near, far in (
            (0, jnp.logical_not(last_of_tile), cross_right),
            (1, jnp.logical_not(first_of_tile), cross_left),
        ):

            @pl.when(near)
            def _():
                settle_send(edge_left.at[it, 0], edge_send.at[it, side_of])

            @pl.when(far)
            def _():
                settle_send(edge_left.at[it, pl.ds(0, lines)], edge_send.at[it, side_of])

        if it == 0:
            for side_of in range(2):

                @pl.when(halo_sends[side_of])
                def _():
                    settle_send(halo_source, halo_send.at[side_of])

        @pl.when(jnp.logical_not(is_dense))
        def _():
            settle_send(shards(near_bands[it], 0, dense_chips * CORES), band_send.at[it])

        @pl.when(is_dense)
        def _():
            settle_send(shards(near_bands[it], 0, (dense_chips - 1) * CORES + 1), band_send.at[it])
            settle_send(shards(near_bands[it], 0, cols - 1), pass_send.at[it])
            settle_send(shards(near_windows[it], 0, rows - 1), win_send.at[it])
            settle_send(shards(near_windows[it], 0, rows - 1), win_pass.at[it])
            settle_send(mix_out.at[it], mix_send.at[it])
            settle_send(zone_out.at[it, :, pl.ds(0, rows - 1)], zone_send.at[it])
            settle_send(pair_out.at[it], pair_send.at[it])
            settle_send(row_out.at[it, :, pl.ds(0, chips - 1)], row_send.at[it])

            @pl.when(c != 0)
            def _():
                settle_send(total_out.at[it], total_send.at[it])

    for it in range(ITERS):
        for p in range(per_shard):
            rounded = traces_ref[:, p * tile : (p + 1) * tile].astype(BF16)
            low, high = rounded[:, :wide], rounded[:, wide:]
            near_bands[it][c * per_shard + p] = jnp.where(core == 0, low, high)
            far_bands[it][c * per_shard + p] = jnp.where(core == 0, high, low)
            top[:, LANES + p * tile : LANES + (p + 1) * tile] = rounded.astype(F32)
            if p == per_shard - 1:
                edge_out[it, 0] = rounded[:, tile - LANES :]
            if p == 0:
                edge_out[it, 1] = rounded[:, :LANES]

        @pl.when(jnp.logical_not(last_of_tile))
        def _():
            edge_near(it, 0).start()

        @pl.when(jnp.logical_not(first_of_tile))
        def _():
            edge_near(it, 1).start()

        @pl.when(cross_right)
        def _():
            for z in range(lines):
                edge_far(it, 0, z).start()

        @pl.when(cross_left)
        def _():
            for z in range(lines):
                edge_far(it, 1, z).start()

        if it == 0:
            for side_of in range(2):

                @pl.when(halo_sends[side_of])
                def _():
                    for kind in range(2):
                        halo_copy(kind, side_of).start()

        for k in near_first:

            @pl.when(peer_chip(k) < dense_chips)
            def _():
                for part in band_copies(it, k):
                    part.start()

        @pl.when(is_dense)
        def _():
            for part in partner_copies(it):
                part.start()

        @pl.when(c == 0)
        def _():
            send_window(it)

        if it == 0:
            prepare_volume()

        @pl.when(is_dense)
        def _():
            dense_part(it)

        @pl.when(jnp.logical_not(is_dense))
        def _():
            gather_top(it)
            relax_groups(it, 0, rhs // SUB)

        if it == 0:
            input_copy(3).wait()
        middle_ref[...] = traces_ref[...] + COUPLING_STEP * (load_ref[...] - traces_ref[...])
        if it == ITERS - 1:
            output_copy(0).start()
            output_copy(2).start()
            for done in range(ITERS):
                drain(done)

        def own(h, p):
            return slice(p * tile + h * wide, p * tile + (h + 1) * wide)

        @pl.when(is_dense)
        def _():
            for h in range(2):
                for p in range(per_shard):
                    product_ref[:, own(h, p)] = row_own[h, chip, p]

        @pl.when(jnp.logical_not(is_dense))
        def _():
            product_ref[...] = jnp.zeros((rhs, shard), F32)

        @pl.when(is_dense)
        def _():
            settle(row_in.at[it, :, pl.ds(0, dense_chips - 1)], row_recv.at[it])

        @pl.when(jnp.logical_not(is_dense))
        def _():
            settle(row_in.at[it, :, pl.ds(0, dense_chips)], row_recv.at[it])

        for src in range(dense_chips):

            @pl.when(src != chip)
            def _():
                for h in range(2):
                    for p in range(per_shard):
                        product_ref[:, own(h, p)] += row_in[it, h, src, p].astype(F32)

        @pl.when(c == 0)
        def _():
            settle(total_in.at[it, pl.ds(0, dense - 1)], total_recv.at[it])
            for p in range(half):
                at = slice(p * tile, (p + 1) * tile)
                product_ref[:, at] += total_own[p]
            for src in range(1, dense):
                for p in range(half):
                    at = (src % CORES) * half + p
                    at = slice(at * tile, (at + 1) * tile)
                    product_ref[:, at] += total_in[it, src, p].astype(F32)

        if it < ITERS - 1:
            change = COUPLING_STEP * (product_ref[...] + flux[...])
            traces_ref[...] = middle_ref[...] - change

    output_copy(1).start()
    for i in range(len(outputs)):
        output_copy(i).wait()


def local(
    trace_start, surface_load, panel_tiles, tile_list, surf_map, coef_index, coef_table, vol_source
):
    cols = lax.axis_size("col")
    rows = lax.axis_size("row")
    lines, layers, nodes = coef_index.shape
    slots, tile, _ = panel_tiles.shape
    rhs, shard = trace_start.shape
    per_shard = shard // tile
    levels = coef_table.shape[0]
    half = per_shard // CORES
    chips = cols // CORES
    span = shard + 2 * LANES
    turns = min(slots, TURNED_BYTES // (2 * tile * tile) - slots)
    cfg = (cols, rows, lines, per_shard, tile, slots, nodes, layers, rhs, levels, turns)
    hbm = pl.BlockSpec(memory_space=pl.ANY)
    block = (rhs, tile)
    piece = (rhs, tile // 2)
    dma = pltpu.SemaphoreType.DMA
    out = jax.ShapeDtypeStruct((rhs, shard), F32)
    middle, product, flux = pl.pallas_call(
        functools.partial(kernel, cfg),
        out_shape=(out,) * 3,
        in_specs=[hbm] * 8,
        out_specs=(hbm,) * 3,
        scratch_shapes=[
            pltpu.VMEM((rhs, shard), F32),
            pltpu.VMEM((rhs, shard), F32),
            pltpu.VMEM((rhs, shard), F32),
            pltpu.SMEM(tile_list.shape, I32),
            pltpu.SMEM(surf_map.shape, I32),
            pltpu.SMEM(coef_table.shape, F32),
            pltpu.VMEM((slots, tile, tile), BF16),
            pltpu.VMEM((turns, tile, tile), BF16),
            pltpu.VMEM((rhs, shard), F32),
            pltpu.VMEM((rhs, shard), F32),
            pltpu.VMEM((lines, layers, nodes), I32),
            pltpu.VMEM((lines, layers, nodes), F32),
            pltpu.VMEM((SUB, LANES), I32),
            pltpu.SMEM((SUB, LANES), I32),
            pltpu.VMEM((cols * per_shard,) + piece, BF16),
            pltpu.VMEM((cols * per_shard,) + piece, BF16),
            pltpu.VMEM((cols * per_shard,) + piece, BF16),
            pltpu.VMEM((cols * per_shard,) + piece, BF16),
            pltpu.VMEM((rows * per_shard,) + piece, BF16),
            pltpu.VMEM((rows * per_shard,) + piece, BF16),
            pltpu.VMEM((rows * per_shard,) + piece, BF16),
            pltpu.VMEM((rows * per_shard,) + piece, BF16),
            pltpu.VMEM((ITERS, 2, rhs, LANES), BF16),
            pltpu.VMEM((ITERS, lines + 1, rhs, LANES), BF16),
            pltpu.VMEM((ITERS, lines + 1, rhs, LANES), BF16),
            pltpu.VMEM((2, lines, layers, LANES), I32),
            pltpu.VMEM((2, lines, layers, LANES), F32),
            pltpu.VMEM((slots + 1,) + block, F32),
            pltpu.VMEM((ITERS, 2, rows, half) + piece, BF16),
            pltpu.VMEM((ITERS, 2, rows, half) + piece, BF16),
            pltpu.VMEM((2, rows, half) + piece, F32),
            pltpu.VMEM((ITERS, 2, rows, half) + piece, BF16),
            pltpu.VMEM((ITERS, 2, rows, half) + piece, BF16),
            pltpu.VMEM((half,) + block, F32),
            pltpu.VMEM((ITERS, half) + block, BF16),
            pltpu.VMEM((ITERS, cols, half) + block, BF16),
            pltpu.VMEM((ITERS, 2, chips, per_shard) + piece, BF16),
            pltpu.VMEM((ITERS, 2, chips, per_shard) + piece, BF16),
            pltpu.VMEM((2, chips, per_shard) + piece, F32),
            pltpu.VMEM((ITERS, 2, chips, per_shard) + piece, BF16),
            pltpu.VMEM((ITERS, 2, chips, per_shard) + piece, BF16),
            pltpu.VMEM((layers, span), I32),
            pltpu.VMEM((layers, span), F32),
            pltpu.VMEM((layers, span), F32),
            pltpu.VMEM((5, layers, SUB, span), F32),
            pltpu.VMEM((2, layers, rhs, span), F32),
            pltpu.VMEM((rhs, span), F32),
            dma((3,)),
            dma((7,)),
            dma((3,)),
            dma,
            dma((ITERS,)),
            dma((ITERS,)),
            dma((ITERS, chips)),
            dma((ITERS,)),
            dma((ITERS,)),
            dma((ITERS,)),
            dma((ITERS, rows)),
            dma((ITERS,)),
            dma((ITERS, 2)),
            dma((ITERS, 2)),
            dma((2,)),
            dma((2,)),
            dma((ITERS,)),
            dma((ITERS, 2)),
            dma((ITERS,)),
            dma((ITERS,)),
            dma((ITERS,)),
            dma((ITERS,)),
            dma((ITERS,)),
            dma((ITERS, 2)),
            dma((ITERS,)),
            dma((ITERS,)),
        ],
        compiler_params=pltpu.CompilerParams(
            collective_id=0, has_side_effects=True, vmem_limit_bytes=60 * 1024 * 1024
        ),
        name="coupled",
    )(
        tile_list,
        surf_map,
        coef_table,
        trace_start,
        surface_load,
        coef_index,
        vol_source,
        panel_tiles,
    )
    response = product + flux
    return middle - COUPLING_STEP * response, response


def solution(mesh):
    return jax.shard_map(
        local,
        mesh=mesh,
        in_specs=(
            P(None, ("col", "row")),
            P(None, ("col", "row")),
            P(("col", "row"), None, None),
            P(("col", "row")),
            P(),
            P(None, None, "row"),
            P(),
            P(None, None, "row"),
        ),
        out_specs=(P(None, ("col", "row")), P(None, ("col", "row"))),
        check_vma=False,
    )
```

time: 51.8 us -> 44.4 us (0.86)
  Pallas kernels: 47.8 us -> 41.8 us
  local copies, waits for them, and re-layouts: 3.14 us -> 0 us
  other arithmetic: 0 us -> 1.76 us
    pallas_call x1, Pallas kernels: 47.8 us -> 41.8 us  [local(): pl.pallas_call(functools.partial(kernel, cfg), out_shape=(out,) * 3, in_s...]
    unnamed x2 -> x0, local copies, waits for them, and re-layouts: 3.14 us -> none
    sub x0 -> x1, other arithmetic: none -> 1.76 us  [local(): return (middle - COUPLING_STEP * response, response)]
where the time goes in v2:
time: 44.4 us; the launch traced here: 44.2 us
  Pallas kernels  41.8 us (94%)
  other arithmetic  1.76 us (4%)
  between operations  0.64 us (1%)
    pallas_call x1, Pallas kernels, local(): pl.pallas_call(functools.partial(kernel, cfg), out_shape=(out,) * 3, in_s...  41.8 us
    sub x1, other arithmetic, local(): return (middle - COUPLING_STEP * response, response)  1.76 us

profile of v2, /device:TPU:0, one launch (start us, length us, event | category | flops | bytes accessed | tf_op | source)
XLA Modules:
  0.0 44.2 jit_solution(14054273695651592509)
XLA Ops:
  0.6 41.8 %coupled.1 = (f32[32,1024]{1,0:T(8,128)}, f32[32,1024]{1,0:T(8,128)}, f32[32,1024]{1,0:T(8,128)}) custom-call(s32[22]{0:T(128)} %list_hbm.1, s32[8]{0:T(128)} %surf_hbm.1, f32[16]{0:T(128)} %table_hbm.1, f32[32,1024]{1,0:T(8,128)} %start_hbm.1, f32[32,1024]{1,0:T(8,128)} %load_hbm.1, s32[2,4,4096]{2,1,0:T(4,128)} %index_hbm.1, f32[2,4,4096]{2,1,0:T(4,128)} %source_hbm.1, ...), custom_call_target="tpu_custom_call" | custom-call | tf_op jit(solution)/shard_map/coupled/pallas_call | solution.py:898
  42.4 1.8 %multiply_subtract_fusion = (f32[32,1024]{1,0:T(8,128)}, f32[32,1024]{1,0:T(8,128)}) fusion(f32[32,1024]{1,0:T(8,128)} %get-tuple-element.5, f32[32,1024]{1,0:T(8,128)} %get-tuple-element.6, f32[32,1024]{1,0:T(8,128)} %get-tuple-element.7), kind=kLoop, calls=%fused_computation | loop fusion | flops 98304 | bytes 655360 | tf_op jit(solution)/shard_map/sub | solution.py:993

commit v3 on v2

--- a/solution.py
+++ b/solution.py
@@ -160,7 +160,7 @@
             device_id_type=pl.DeviceIdType.MESH,
         )
 
-    stops = sorted({0, slots // 4, slots // 2 // 2 * 2, slots})
+    stops = sorted({0, slots * 3 // 8, slots * 3 // 4, slots})
 
     def panel_copy(i):
         part = pl.ds(stops[i], stops[i + 1] - stops[i])
@@ -191,6 +191,7 @@
             barrier, inc=1, device_id=(to_col, to_row), device_id_type=pl.DeviceIdType.MESH
         )
 
+    input_copy(0).start()
     for k in range(1, rows):
         greet(c, lax.rem(r + k, rows))
     for k in range(1, cols):
@@ -206,7 +207,7 @@
         for z in range(lines):
             greet(z * group + group - 1, row_down)
 
-    for i in (4, 0, 1, 2, 5, 6, 3):
+    for i in (1, 2, 4, 5, 6, 3):
         input_copy(i).start()
 
     @pl.when(is_dense)
@@ -264,20 +265,7 @@
             for i, x in enumerate((place, origin, jnp.where(keep, 1, 0), last)):
                 tab[4 * which + i : 4 * which + i + 1, :] = x[0:1, :]
 
-    input_copy(4).wait()
-
-    @pl.when(is_dense)
-    def _():
-        sort_slots()
-        pltpu.make_async_copy(tab, order, tab_sem).start()
-        product[slots] = jnp.zeros((rhs, tile), F32)
-
     input_copy(0).wait()
-    input_copy(1).wait()
-    input_copy(2).wait()
-    input_copy(5).wait()
-    input_copy(6).wait()
-
     expected = (
         cols - 1 + rows - 1 + jnp.where(cross_right, lines, 0) + jnp.where(cross_left, lines, 0)
     )
@@ -337,7 +325,8 @@
     bits = chips.bit_length() - 1
     power = chips == 1 << bits
     near_first = sorted(range(1, chips), key=lambda k: k.bit_count() if power else k)
-    far_first = near_first[::-1]
+    beside = [k for k in near_first if power and k.bit_count() == 1]
+    beyond = [k for k in near_first if k not in beside]
 
     def peer_chip(k):
         if not power:
@@ -358,8 +347,8 @@
             copy(near, far, pass_send.at[it], far_recv.at[it], partner, r),
         )
 
-    def band_pass(it, k):
-        at = peer_chip(k) * CORES
+    def band_pass(it, peer):
+        at = peer * CORES
         return copy(
             shards(near_bands[it], at, CORES),
             shards(far_bands[it], at, CORES),
@@ -616,7 +605,7 @@
                 value = row_own[h, k, p] + pair_in[it, h, k, p].astype(F32)
                 row_own[h, k, p] = value
                 row_out[it, h, k, p] = value.astype(BF16)
-        for k in far_first:
+        for k in near_first if h == 0 and it < ITERS - 1 else beside:
             row_copy(it, h, k).start()
 
     def wait_panel():
@@ -640,6 +629,26 @@
         lax.fori_loop(0, (end - begin) // 2, two, 0)
         if (end - begin) % 2:
             one(end - 1)
+
+    def begin():
+        input_copy(1).wait()
+        input_copy(2).wait()
+        for side_of in range(2):
+
+            @pl.when(halo_sends[side_of])
+            def _():
+                for kind in range(2):
+                    halo_copy(kind, side_of).start()
+
+        input_copy(4).wait()
+        input_copy(5).wait()
+        input_copy(6).wait()
+
+        @pl.when(is_dense)
+        def _():
+            sort_slots()
+            pltpu.make_async_copy(tab, order, tab_sem).start()
+            product[slots] = jnp.zeros((rhs, tile), F32)
 
     def dense_part(it):
         near_band, far_band = near_bands[it], far_bands[it]
@@ -650,22 +659,31 @@
                 wait_panel()
             for i in range(len(stops) - 2):
                 turn(i)
+            prepare_volume()
         settle(shards(near_band, partner), near_recv.at[it, chip])
 
         @pl.when(c == 1)
         def _():
             send_window(it)
 
-        for i, k in enumerate(near_first):
-            settle(shards(near_band, peer_chip(k) * CORES, CORES), near_recv.at[it, peer_chip(k)])
-            band_pass(it, k).start()
-
-            @pl.when(peer_chip(k) == 0)
-            def _():
-                send_window(it)
-
-            if it == 0 and i == min(1, len(near_first) - 1):
-                turn(len(stops) - 2)
+        def pass_on(peer):
+            settle(shards(near_band, peer * CORES, CORES), near_recv.at[it, peer])
+            band_pass(it, peer).start()
+
+        @pl.when(chip != 0)
+        def _():
+            settle(shards(near_band, 0, CORES), near_recv.at[it, 0])
+            send_window(it)
+            band_pass(it, 0).start()
+
+        if it == 0:
+            turn(len(stops) - 2)
+        for k in near_first:
+            peer = peer_chip(k)
+
+            @pl.when(peer != 0)
+            def _():
+                pass_on(peer)
 
         if it == 0 and turns == slots:
             pltpu.make_async_copy(tab, order, tab_sem).wait()
@@ -678,12 +696,15 @@
         segments(0, far_band, other, 1)
         send_mix(it, 1)
         send_zone(it, 0)
-        send_zone(it, 1)
+        if it > 0:
+            send_zone(it, 1)
         for k in range(1, rows):
             at = lax.rem(r + k, rows)
             settle(shards(near_window, at), win_recv.at[it, at])
             window_pass(it, at).start()
         segments(1, near_window, core)
+        if it == 0:
+            send_zone(it, 1)
         settle(shards(far_window, 0, rows - 1), win_far.at[it])
         segments(1, far_window, other, 0)
         send_pair(it, 0)
@@ -708,6 +729,9 @@
         def _():
             total_copy(it).start()
 
+        for h in range(0 if it == ITERS - 1 else 1, 2):
+            for k in beyond:
+                row_copy(it, h, k).start()
         relax_groups(it, groups // 2, groups)
 
     def drain(it):
@@ -780,14 +804,6 @@
             for z in range(lines):
                 edge_far(it, 1, z).start()
 
-        if it == 0:
-            for side_of in range(2):
-
-                @pl.when(halo_sends[side_of])
-                def _():
-                    for kind in range(2):
-                        halo_copy(kind, side_of).start()
-
         for k in near_first:
 
             @pl.when(peer_chip(k) < dense_chips)
@@ -805,7 +821,7 @@
             send_window(it)
 
         if it == 0:
-            prepare_volume()
+            begin()
 
         @pl.when(is_dense)
         def _():
@@ -813,6 +829,8 @@
 
         @pl.when(jnp.logical_not(is_dense))
         def _():
+            if it == 0:
+                prepare_volume()
             gather_top(it)
             relax_groups(it, 0, rhs // SUB)
 

time: 44.4 us -> 41.4 us (0.932)
  Pallas kernels: 41.8 us -> 38.9 us
    pallas_call x1, Pallas kernels: 41.8 us -> 38.9 us  [local(): pl.pallas_call(functools.partial(kernel, cfg), out_shape=(out,) * 3, in_s...]
where the time goes in v3:
time: 41.4 us; the launch traced here: 41.3 us
  Pallas kernels  38.9 us (94%)
  other arithmetic  1.76 us (4%)
  between operations  0.64 us (2%)
    pallas_call x1, Pallas kernels, local(): pl.pallas_call(functools.partial(kernel, cfg), out_shape=(out,) * 3, in_s...  38.9 us
    sub x1, other arithmetic, local(): return (middle - COUPLING_STEP * response, response)  1.76 us

profile of v3, /device:TPU:0, one launch (start us, length us, event | category | flops | bytes accessed | tf_op | source)
XLA Modules:
  0.0 41.3 jit_solution(8615358245159712402)
XLA Ops:
  0.6 38.9 %coupled.1 = (f32[32,1024]{1,0:T(8,128)}, f32[32,1024]{1,0:T(8,128)}, f32[32,1024]{1,0:T(8,128)}) custom-call(s32[22]{0:T(128)} %list_hbm.1, s32[8]{0:T(128)} %surf_hbm.1, f32[16]{0:T(128)} %table_hbm.1, f32[32,1024]{1,0:T(8,128)} %start_hbm.1, f32[32,1024]{1,0:T(8,128)} %load_hbm.1, s32[2,4,4096]{2,1,0:T(4,128)} %index_hbm.1, f32[2,4,4096]{2,1,0:T(4,128)} %source_hbm.1, ...), custom_call_target="tpu_custom_call" | custom-call | tf_op jit(solution)/shard_map/coupled/pallas_call | solution.py:916
  39.5 1.8 %multiply_subtract_fusion = (f32[32,1024]{1,0:T(8,128)}, f32[32,1024]{1,0:T(8,128)}) fusion(f32[32,1024]{1,0:T(8,128)} %get-tuple-element.5, f32[32,1024]{1,0:T(8,128)} %get-tuple-element.6, f32[32,1024]{1,0:T(8,128)} %get-tuple-element.7), kind=kLoop, calls=%fused_computation | loop fusion | flops 98304 | bytes 655360 | tf_op jit(solution)/shard_map/sub | solution.py:1011

commit v4 on v3

--- a/solution.py
+++ b/solution.py
@@ -269,7 +269,6 @@
     expected = (
         cols - 1 + rows - 1 + jnp.where(cross_right, lines, 0) + jnp.where(cross_left, lines, 0)
     )
-    pl.semaphore_wait(barrier, expected)
 
     def settle(ref, sem):
         copy(ref, ref, sem, sem, partner, r).wait_recv()
@@ -403,14 +402,19 @@
             zone_out.at[it, h, peer],
             zone_in.at[it, h, r],
             zone_send.at[it],
-            zone_recv.at[it],
+            zone_recv.at[it, h],
             c,
             peer,
         )
 
-    def total_copy(it):
+    def total_copy(it, h):
         return copy(
-            total_out.at[it], total_in.at[it, c], total_send.at[it], total_recv.at[it], 0, r
+            total_out.at[it, h],
+            total_in.at[it, h, c],
+            total_send.at[it],
+            total_recv.at[it, h],
+            0,
+            r,
         )
 
 
@@ -430,7 +434,7 @@
             row_out.at[it, h, peer],
             row_in.at[it, h, chip],
             row_send.at[it],
-            row_recv.at[it],
+            row_recv.at[it, h],
             peer * CORES + core,
             r,
         )
@@ -649,6 +653,19 @@
             sort_slots()
             pltpu.make_async_copy(tab, order, tab_sem).start()
             product[slots] = jnp.zeros((rhs, tile), F32)
+
+    def send_total(it, h):
+        settle(zone_in.at[it, h, pl.ds(0, rows - 1)], zone_recv.at[it, h])
+        for p in range(half):
+            value = zone_own[h, r, p]
+            for k in range(1, rows):
+                value = value + zone_in[it, h, lax.rem(r + k, rows), p].astype(F32)
+            total_own[h, p] = value
+            total_out[it, h, p] = value.astype(BF16)
+
+        @pl.when(c != 0)
+        def _():
+            total_copy(it, h).start()
 
     def dense_part(it):
         near_band, far_band = near_bands[it], far_bands[it]
@@ -716,19 +733,8 @@
         send_rows(it, 0)
         relax_groups(it, groups // 4, groups // 2)
         send_rows(it, 1)
-        settle(zone_in.at[it, :, pl.ds(0, rows - 1)], zone_recv.at[it])
-        for p in range(half):
-            for h in range(2):
-                value = zone_own[h, r, p]
-                for k in range(1, rows):
-                    value = value + zone_in[it, h, lax.rem(r + k, rows), p].astype(F32)
-                total_own[p, :, lanes_of(h)] = value
-                total_out[it, p, :, lanes_of(h)] = value.astype(BF16)
-
-        @pl.when(c != 0)
-        def _():
-            total_copy(it).start()
-
+        for h in range(2):
+            send_total(it, h)
         for h in range(0 if it == ITERS - 1 else 1, 2):
             for k in beyond:
                 row_copy(it, h, k).start()
@@ -774,54 +780,105 @@
             def _():
                 settle_send(total_out.at[it], total_send.at[it])
 
+    def own(h, p):
+        return slice(p * tile + h * wide, p * tile + (h + 1) * wide)
+
+    def round_half(it, h):
+        for p in range(per_shard):
+            rounded = traces_ref[:, own(h, p)].astype(BF16)
+
+            @pl.when(core == h)
+            def _():
+                near_bands[it][c * per_shard + p] = rounded
+
+            @pl.when(core != h)
+            def _():
+                far_bands[it][c * per_shard + p] = rounded
+
+            at = LANES + p * tile + h * wide
+            top[:, at : at + wide] = rounded.astype(F32)
+            if h == 1 and p == per_shard - 1:
+                edge_out[it, 0] = rounded[:, wide - LANES :]
+            if h == 0 and p == 0:
+                edge_out[it, 1] = rounded[:, :LANES]
+
+    def send_half(it, h):
+        side_of = 1 - h
+        inner, outer = ((last_of_tile, cross_right), (first_of_tile, cross_left))[side_of]
+
+        @pl.when(jnp.logical_not(inner))
+        def _():
+            edge_near(it, side_of).start()
+
+        @pl.when(outer)
+        def _():
+            for z in range(lines):
+                edge_far(it, side_of, z).start()
+
+        for k in near_first:
+            same, cross = band_copies(it, k)
+
+            @pl.when((peer_chip(k) < dense_chips) & (core == h))
+            def _():
+                same.start()
+
+            @pl.when((peer_chip(k) < dense_chips) & (core != h))
+            def _():
+                cross.start()
+
+        to_near, to_far = partner_copies(it)
+
+        @pl.when(is_dense & (core == h))
+        def _():
+            to_far.start()
+
+        @pl.when(is_dense & (core != h))
+        def _():
+            to_near.start()
+
+        if h == 0:
+
+            @pl.when(c == 0)
+            def _():
+                send_window(it)
+
+    def finish_half(it, h):
+        @pl.when(is_dense)
+        def _():
+            for p in range(per_shard):
+                product_ref[:, own(h, p)] = row_own[h, chip, p]
+            settle(row_in.at[it, h, pl.ds(0, dense_chips - 1)], row_recv.at[it, h])
+
+        @pl.when(jnp.logical_not(is_dense))
+        def _():
+            for p in range(per_shard):
+                product_ref[:, own(h, p)] = jnp.zeros((rhs, wide), F32)
+            settle(row_in.at[it, h, pl.ds(0, dense_chips)], row_recv.at[it, h])
+
+        for src in range(dense_chips):
+
+            @pl.when(src != chip)
+            def _():
+                for p in range(per_shard):
+                    product_ref[:, own(h, p)] += row_in[it, h, src, p].astype(F32)
+
+        @pl.when(c == 0)
+        def _():
+            settle(total_in.at[it, h, pl.ds(0, dense - 1)], total_recv.at[it, h])
+            for p in range(half):
+                product_ref[:, own(h, p)] += total_own[h, p]
+            for src in range(1, dense):
+                for p in range(half):
+                    at = own(h, (src % CORES) * half + p)
+                    product_ref[:, at] += total_in[it, h, src, p].astype(F32)
+
+    for h in range(2):
+        round_half(0, h)
+    pl.semaphore_wait(barrier, expected)
+    for h in range(2):
+        send_half(0, h)
+    begin()
     for it in range(ITERS):
-        for p in range(per_shard):
-            rounded = traces_ref[:, p * tile : (p + 1) * tile].astype(BF16)
-            low, high = rounded[:, :wide], rounded[:, wide:]
-            near_bands[it][c * per_shard + p] = jnp.where(core == 0, low, high)
-            far_bands[it][c * per_shard + p] = jnp.where(core == 0, high, low)
-            top[:, LANES + p * tile : LANES + (p + 1) * tile] = rounded.astype(F32)
-            if p == per_shard - 1:
-                edge_out[it, 0] = rounded[:, tile - LANES :]
-            if p == 0:
-                edge_out[it, 1] = rounded[:, :LANES]
-
-        @pl.when(jnp.logical_not(last_of_tile))
-        def _():
-            edge_near(it, 0).start()
-
-        @pl.when(jnp.logical_not(first_of_tile))
-        def _():
-            edge_near(it, 1).start()
-
-        @pl.when(cross_right)
-        def _():
-            for z in range(lines):
-                edge_far(it, 0, z).start()
-
-        @pl.when(cross_left)
-        def _():
-            for z in range(lines):
-                edge_far(it, 1, z).start()
-
-        for k in near_first:
-
-            @pl.when(peer_chip(k) < dense_chips)
-            def _():
-                for part in band_copies(it, k):
-                    part.start()
-
-        @pl.when(is_dense)
-        def _():
-            for part in partner_copies(it):
-                part.start()
-
-        @pl.when(c == 0)
-        def _():
-            send_window(it)
-
-        if it == 0:
-            begin()
 
         @pl.when(is_dense)
         def _():
@@ -842,51 +899,15 @@
             output_copy(2).start()
             for done in range(ITERS):
                 drain(done)
-
-        def own(h, p):
-            return slice(p * tile + h * wide, p * tile + (h + 1) * wide)
-
-        @pl.when(is_dense)
-        def _():
-            for h in range(2):
+        for h in range(2):
+            finish_half(it, h)
+            if it < ITERS - 1:
                 for p in range(per_shard):
-                    product_ref[:, own(h, p)] = row_own[h, chip, p]
-
-        @pl.when(jnp.logical_not(is_dense))
-        def _():
-            product_ref[...] = jnp.zeros((rhs, shard), F32)
-
-        @pl.when(is_dense)
-        def _():
-            settle(row_in.at[it, :, pl.ds(0, dense_chips - 1)], row_recv.at[it])
-
-        @pl.when(jnp.logical_not(is_dense))
-        def _():
-            settle(row_in.at[it, :, pl.ds(0, dense_chips)], row_recv.at[it])
-
-        for src in range(dense_chips):
-
-            @pl.when(src != chip)
-            def _():
-                for h in range(2):
-                    for p in range(per_shard):
-                        product_ref[:, own(h, p)] += row_in[it, h, src, p].astype(F32)
-
-        @pl.when(c == 0)
-        def _():
-            settle(total_in.at[it, pl.ds(0, dense - 1)], total_recv.at[it])
-            for p in range(half):
-                at = slice(p * tile, (p + 1) * tile)
-                product_ref[:, at] += total_own[p]
-            for src in range(1, dense):
-                for p in range(half):
-                    at = (src % CORES) * half + p
-                    at = slice(at * tile, (at + 1) * tile)
-                    product_ref[:, at] += total_in[it, src, p].astype(F32)
-
-        if it < ITERS - 1:
-            change = COUPLING_STEP * (product_ref[...] + flux[...])
-            traces_ref[...] = middle_ref[...] - change
+                    at = own(h, p)
+                    change = COUPLING_STEP * (product_ref[:, at] + flux[:, at])
+                    traces_ref[:, at] = middle_ref[:, at] - change
+                round_half(it + 1, h)
+                send_half(it + 1, h)
 
     output_copy(1).start()
     for i in range(len(outputs)):
@@ -952,9 +973,9 @@
             pltpu.VMEM((2, rows, half) + piece, F32),
             pltpu.VMEM((ITERS, 2, rows, half) + piece, BF16),
             pltpu.VMEM((ITERS, 2, rows, half) + piece, BF16),
-            pltpu.VMEM((half,) + block, F32),
-            pltpu.VMEM((ITERS, half) + block, BF16),
-            pltpu.VMEM((ITERS, cols, half) + block, BF16),
+            pltpu.VMEM((2, half) + piece, F32),
+            pltpu.VMEM((ITERS, 2, half) + piece, BF16),
+            pltpu.VMEM((ITERS, 2, cols, half) + piece, BF16),
             pltpu.VMEM((ITERS, 2, chips, per_shard) + piece, BF16),
             pltpu.VMEM((ITERS, 2, chips, per_shard) + piece, BF16),
             pltpu.VMEM((2, chips, per_shard) + piece, F32),
@@ -985,13 +1006,13 @@
             dma((ITERS,)),
             dma((ITERS, 2)),
             dma((ITERS,)),
-            dma((ITERS,)),
-            dma((ITERS,)),
-            dma((ITERS,)),
+            dma((ITERS, 2)),
             dma((ITERS,)),
             dma((ITERS, 2)),
             dma((ITERS,)),
+            dma((ITERS, 2)),
             dma((ITERS,)),
+            dma((ITERS, 2)),
         ],
         compiler_params=pltpu.CompilerParams(
             collective_id=0, has_side_effects=True, vmem_limit_bytes=60 * 1024 * 1024

time: 41.4 us -> 40.5 us (0.978)
  Pallas kernels: 38.9 us -> 38 us
    pallas_call x1, Pallas kernels: 38.9 us -> 38 us  [local(): pl.pallas_call(functools.partial(kernel, cfg), out_shape=(out,) * 3, in_s...]
where the time goes in v4:
time: 40.5 us; the launch traced here: 40.3 us
  Pallas kernels  38 us (94%)
  other arithmetic  1.76 us (4%)
  between operations  0.64 us (2%)
    pallas_call x1, Pallas kernels, local(): pl.pallas_call(functools.partial(kernel, cfg), out_shape=(out,) * 3, in_s...  38 us
    sub x1, other arithmetic, local(): return (middle - COUPLING_STEP * response, response)  1.76 us

profile of v4, /device:TPU:0, one launch (start us, length us, event | category | flops | bytes accessed | tf_op | source)
XLA Modules:
  0.0 40.3 jit_solution(15074633059913209811)
XLA Ops:
  0.6 38.0 %coupled.1 = (f32[32,1024]{1,0:T(8,128)}, f32[32,1024]{1,0:T(8,128)}, f32[32,1024]{1,0:T(8,128)}) custom-call(s32[22]{0:T(128)} %list_hbm.1, s32[8]{0:T(128)} %surf_hbm.1, f32[16]{0:T(128)} %table_hbm.1, f32[32,1024]{1,0:T(8,128)} %start_hbm.1, f32[32,1024]{1,0:T(8,128)} %load_hbm.1, s32[2,4,4096]{2,1,0:T(4,128)} %index_hbm.1, f32[2,4,4096]{2,1,0:T(4,128)} %source_hbm.1, ...), custom_call_target="tpu_custom_call" | custom-call | tf_op jit(solution)/shard_map/coupled/pallas_call | solution.py:937
  38.6 1.8 %multiply_subtract_fusion = (f32[32,1024]{1,0:T(8,128)}, f32[32,1024]{1,0:T(8,128)}) fusion(f32[32,1024]{1,0:T(8,128)} %get-tuple-element.5, f32[32,1024]{1,0:T(8,128)} %get-tuple-element.6, f32[32,1024]{1,0:T(8,128)} %get-tuple-element.7), kind=kLoop, calls=%fused_computation | loop fusion | flops 98304 | bytes 655360 | tf_op jit(solution)/shard_map/sub | solution.py:1032

commit v5 on v4

--- a/solution.py
+++ b/solution.py
@@ -100,7 +100,6 @@
     near_recv,
     far_recv,
     win_send,
-    win_pass,
     win_recv,
     win_far,
     edge_send,
@@ -373,7 +372,7 @@
             shards(near_bands[it], 0),
             shards(near_windows[it], r),
             win_send.at[it],
-            win_recv.at[it, r],
+            win_recv.at[it],
             c,
             peer,
         )
@@ -382,7 +381,7 @@
         return copy(
             shards(near_windows[it], at),
             shards(far_windows[it], at),
-            win_pass.at[it],
+            win_send.at[it],
             win_far.at[it],
             partner,
             r,
@@ -715,10 +714,9 @@
         send_zone(it, 0)
         if it > 0:
             send_zone(it, 1)
+        settle(shards(near_window, 0, rows - 1), win_recv.at[it])
         for k in range(1, rows):
-            at = lax.rem(r + k, rows)
-            settle(shards(near_window, at), win_recv.at[it, at])
-            window_pass(it, at).start()
+            window_pass(it, lax.rem(r + k, rows)).start()
         segments(1, near_window, core)
         if it == 0:
             send_zone(it, 1)
@@ -769,8 +767,7 @@
         def _():
             settle_send(shards(near_bands[it], 0, (dense_chips - 1) * CORES + 1), band_send.at[it])
             settle_send(shards(near_bands[it], 0, cols - 1), pass_send.at[it])
-            settle_send(shards(near_windows[it], 0, rows - 1), win_send.at[it])
-            settle_send(shards(near_windows[it], 0, rows - 1), win_pass.at[it])
+            settle_send(shards(near_bands[it], 0, 2 * (rows - 1)), win_send.at[it])
             settle_send(mix_out.at[it], mix_send.at[it])
             settle_send(zone_out.at[it, :, pl.ds(0, rows - 1)], zone_send.at[it])
             settle_send(pair_out.at[it], pair_send.at[it])
@@ -997,7 +994,6 @@
             dma((ITERS,)),
             dma((ITERS,)),
             dma((ITERS,)),
-            dma((ITERS, rows)),
             dma((ITERS,)),
             dma((ITERS, 2)),
             dma((ITERS, 2)),

time: 40.5 us -> 40.5 us (level)
  no operation moved by 1% of the time
where the time goes in v5:
time: 40.5 us; the launch traced here: 40.3 us
  Pallas kernels  37.9 us (94%)
  other arithmetic  1.76 us (4%)
  between operations  0.64 us (2%)
    pallas_call x1, Pallas kernels, local(): pl.pallas_call(functools.partial(kernel, cfg), out_shape=(out,) * 3, in_s...  37.9 us
    sub x1, other arithmetic, local(): return (middle - COUPLING_STEP * response, response)  1.76 us

profile of v5, /device:TPU:0, one launch (start us, length us, event | category | flops | bytes accessed | tf_op | source)
XLA Modules:
  0.0 40.3 jit_solution(10409270385044794400)
XLA Ops:
  0.6 37.9 %coupled.1 = (f32[32,1024]{1,0:T(8,128)}, f32[32,1024]{1,0:T(8,128)}, f32[32,1024]{1,0:T(8,128)}) custom-call(s32[22]{0:T(128)} %list_hbm.1, s32[8]{0:T(128)} %surf_hbm.1, f32[16]{0:T(128)} %table_hbm.1, f32[32,1024]{1,0:T(8,128)} %start_hbm.1, f32[32,1024]{1,0:T(8,128)} %load_hbm.1, s32[2,4,4096]{2,1,0:T(4,128)} %index_hbm.1, f32[2,4,4096]{2,1,0:T(4,128)} %source_hbm.1, ...), custom_call_target="tpu_custom_call" | custom-call | tf_op jit(solution)/shard_map/coupled/pallas_call | solution.py:934
  38.6 1.8 %multiply_subtract_fusion = (f32[32,1024]{1,0:T(8,128)}, f32[32,1024]{1,0:T(8,128)}) fusion(f32[32,1024]{1,0:T(8,128)} %get-tuple-element.5, f32[32,1024]{1,0:T(8,128)} %get-tuple-element.6, f32[32,1024]{1,0:T(8,128)} %get-tuple-element.7), kind=kLoop, calls=%fused_computation | loop fusion | flops 98304 | bytes 655360 | tf_op jit(solution)/shard_map/sub | solution.py:1028

commit v6 on v5

--- a/solution.py
+++ b/solution.py
@@ -106,15 +106,12 @@
     edge_recv,
     halo_send,
     halo_recv,
-    mix_send,
+    sum_send,
     mix_recv,
     zone_send,
     zone_recv,
-    total_send,
     total_recv,
-    pair_send,
     pair_recv,
-    row_send,
     row_recv,
 ):
     cols, rows, lines, per_shard, tile, slots, nodes, layers, rhs, levels, turns = cfg
@@ -181,7 +178,7 @@
     outputs = ((middle_ref, middle_hbm), (product_ref, product_hbm), (flux, flux_hbm))
 
     def output_copy(i):
-        return pltpu.make_async_copy(outputs[i][0], outputs[i][1], output_sem.at[i])
+        return pltpu.make_async_copy(outputs[i][0], outputs[i][1], output_sem)
 
     barrier = pltpu.get_barrier_semaphore()
 
@@ -393,7 +390,7 @@
 
     def mix_copy(it, h):
         return copy(
-            mix_out.at[it, h], mix_in.at[it, h], mix_send.at[it], mix_recv.at[it, h], partner, r
+            mix_out.at[it, h], mix_in.at[it, h], sum_send.at[it], mix_recv.at[it, h], partner, r
         )
 
     def zone_copy(it, h, peer):
@@ -410,7 +407,7 @@
         return copy(
             total_out.at[it, h],
             total_in.at[it, h, c],
-            total_send.at[it],
+            zone_send.at[it],
             total_recv.at[it, h],
             0,
             r,
@@ -421,7 +418,7 @@
         return copy(
             pair_out.at[it, h],
             pair_in.at[it, h],
-            pair_send.at[it],
+            sum_send.at[it],
             pair_recv.at[it, h],
             partner,
             r,
@@ -432,7 +429,7 @@
         return copy(
             row_out.at[it, h, peer],
             row_in.at[it, h, chip],
-            row_send.at[it],
+            sum_send.at[it],
             row_recv.at[it, h],
             peer * CORES + core,
             r,
@@ -768,14 +765,16 @@
             settle_send(shards(near_bands[it], 0, (dense_chips - 1) * CORES + 1), band_send.at[it])
             settle_send(shards(near_bands[it], 0, cols - 1), pass_send.at[it])
             settle_send(shards(near_bands[it], 0, 2 * (rows - 1)), win_send.at[it])
-            settle_send(mix_out.at[it], mix_send.at[it])
-            settle_send(zone_out.at[it, :, pl.ds(0, rows - 1)], zone_send.at[it])
-            settle_send(pair_out.at[it], pair_send.at[it])
-            settle_send(row_out.at[it, :, pl.ds(0, chips - 1)], row_send.at[it])
+            pieces = 2 * (rows * half + (2 * chips - 1) * per_shard)
+            settle_send(product.at[pl.ds(0, pieces // 4)], sum_send.at[it])
+
+            @pl.when(c == 0)
+            def _():
+                settle_send(zone_out.at[it, :, pl.ds(0, rows - 1)], zone_send.at[it])
 
             @pl.when(c != 0)
             def _():
-                settle_send(total_out.at[it], total_send.at[it])
+                settle_send(zone_out.at[it], zone_send.at[it])
 
     def own(h, p):
         return slice(p * tile + h * wide, p * tile + (h + 1) * wide)
@@ -907,8 +906,8 @@
                 send_half(it + 1, h)
 
     output_copy(1).start()
-    for i in range(len(outputs)):
-        output_copy(i).wait()
+    every = product.at[pl.ds(0, len(outputs) * per_shard)]
+    pltpu.make_async_copy(every, every, output_sem).wait()
 
 
 def local(
@@ -924,6 +923,7 @@
     half = per_shard // CORES
     chips = cols // CORES
     span = shard + 2 * LANES
+    assert (rows * half + (2 * chips - 1) * per_shard) % 2 == 0
     turns = min(slots, TURNED_BYTES // (2 * tile * tile) - slots)
     cfg = (cols, rows, lines, per_shard, tile, slots, nodes, layers, rhs, levels, turns)
     hbm = pl.BlockSpec(memory_space=pl.ANY)
@@ -986,7 +986,7 @@
             pltpu.VMEM((rhs, span), F32),
             dma((3,)),
             dma((7,)),
-            dma((3,)),
+            dma,
             dma,
             dma((ITERS,)),
             dma((ITERS,)),
@@ -1003,11 +1003,8 @@
             dma((ITERS, 2)),
             dma((ITERS,)),
             dma((ITERS, 2)),
-            dma((ITERS,)),
             dma((ITERS, 2)),
-            dma((ITERS,)),
             dma((ITERS, 2)),
-            dma((ITERS,)),
             dma((ITERS, 2)),
         ],
         compiler_params=pltpu.CompilerParams(

time: 40.5 us -> 40.4 us (level)
  no operation moved by 1% of the time
where the time goes in v6:
time: 40.4 us; the launch traced here: 40.2 us
  Pallas kernels  37.8 us (94%)
  other arithmetic  1.76 us (4%)
  between operations  0.64 us (2%)
    pallas_call x1, Pallas kernels, local(): pl.pallas_call(functools.partial(kernel, cfg), out_shape=(out,) * 3, in_s...  37.8 us
    sub x1, other arithmetic, local(): return (middle - COUPLING_STEP * response, response)  1.76 us

profile of v6, /device:TPU:0, one launch (start us, length us, event | category | flops | bytes accessed | tf_op | source)
XLA Modules:
  0.0 40.2 jit_solution(2576078056558249004)
XLA Ops:
  0.6 37.8 %coupled.1 = (f32[32,1024]{1,0:T(8,128)}, f32[32,1024]{1,0:T(8,128)}, f32[32,1024]{1,0:T(8,128)}) custom-call(s32[22]{0:T(128)} %list_hbm.1, s32[8]{0:T(128)} %surf_hbm.1, f32[16]{0:T(128)} %table_hbm.1, f32[32,1024]{1,0:T(8,128)} %start_hbm.1, f32[32,1024]{1,0:T(8,128)} %load_hbm.1, s32[2,4,4096]{2,1,0:T(4,128)} %index_hbm.1, f32[2,4,4096]{2,1,0:T(4,128)} %source_hbm.1, ...), custom_call_target="tpu_custom_call" | custom-call | tf_op jit(solution)/shard_map/coupled/pallas_call | solution.py:934
  38.5 1.8 %multiply_subtract_fusion = (f32[32,1024]{1,0:T(8,128)}, f32[32,1024]{1,0:T(8,128)}) fusion(f32[32,1024]{1,0:T(8,128)} %get-tuple-element.5, f32[32,1024]{1,0:T(8,128)} %get-tuple-element.6, f32[32,1024]{1,0:T(8,128)} %get-tuple-element.7), kind=kLoop, calls=%fused_computation | loop fusion | flops 98304 | bytes 655360 | tf_op jit(solution)/shard_map/sub | solution.py:1025
